TPU v7x, 32 devices: a whole 2x2x4 slice. The times are simulated.
32 devices in a mesh: slab: 8 (over y, x, core), cross: 4 (over z).
Axes of the slice: x: 2, y: 2, z: 4, core: 2. Of those that a mesh axis runs over, the one named last changes fastest.
Arguments:
- velocity: float32 [3, 32, 64, 128], P(None, 'slab', 'cross'), may hold values from -6 to 6
- density: float32 [32, 64, 128], P('slab', 'cross'), may hold values from 0.5 to 2
- source: float32 [32, 64, 128], P('slab', 'cross'), may hold values from -6 to 6
- species: float32 [9, 32, 64, 128], P(None, 'slab', 'cross'), may hold values from 0 to 1
Outputs:
- velocity_out: float32 [3, 32, 64, 128], P(None, 'slab', 'cross')
- pressure: float32 [32, 64, 128], P('slab', 'cross')
- species_out: float32 [9, 32, 64, 128], P(None, 'slab', 'cross')
All inputs are finite; a program needn't handle non-finite values.
Results may differ from a plain program's by a relative error of at most 0.0001.
Values sent between devices are 32-bit elements; how exact they have to be, the bound alone decides.
A program may use at most 64 MiB of HBM per device.

v0:
```python
import jax
import jax.numpy as jnp
from jax import lax
from jax.sharding import PartitionSpec as P

CYCLES = 2
COARSE = 4


damping = 0.8
time_step = 0.25


def with_halo(block, sides, width):
    for axis, dim in sides:
        count = lax.axis_size(axis)
        forward = [(i, i + 1) for i in range(count - 1)]
        backward = [(target, source) for source, target in forward]
        low = lax.ppermute(
            lax.slice_in_dim(block, block.shape[dim] - width, None, axis=dim), axis, forward
        )
        high = lax.ppermute(lax.slice_in_dim(block, 0, width, axis=dim), axis, backward)
        block = jnp.concatenate([low, block, high], axis=dim)
    return block


def pad_depth(field):
    return jnp.pad(field, ((0, 0), (0, 0), (1, 1)))


def face_weights(mobile):
    face_x = 0.5 * (mobile[:-1, 1:-1] + mobile[1:, 1:-1])
    face_y = 0.5 * (mobile[1:-1, :-1] + mobile[1:-1, 1:])
    inner = pad_depth(mobile[1:-1, 1:-1])
    face_z = 0.5 * (inner[..., :-1] + inner[..., 1:])
    diagonal = (
        face_x[:-1]
        + face_x[1:]
        + face_y[:, :-1]
        + face_y[:, 1:]
        + face_z[..., :-1]
        + face_z[..., 1:]
    )
    return (face_x, face_y, face_z, diagonal)


def operate(field, weights):
    face_x, face_y, face_z = (weights[0], weights[1], weights[2])
    center = field[1:-1, 1:-1]
    column = pad_depth(center)
    total = face_x[1:] * (field[2:, 1:-1] - center) + face_x[:-1] * (field[:-2, 1:-1] - center)
    total = (
        total
        + face_y[:, 1:] * (field[1:-1, 2:] - center)
        + face_y[:, :-1] * (field[1:-1, :-2] - center)
    )
    total = (
        total
        + face_z[..., 1:] * (column[..., 2:] - center)
        + face_z[..., :-1] * (column[..., :-2] - center)
    )
    return total


def jacobi_step(field, target, weights):
    center = field[1:-1, 1:-1]
    return center + damping * (operate(field, weights) - target) / weights[3]


def divergence(moving):
    column = pad_depth(moving[2][1:-1, 1:-1])
    total = (
        moving[0][2:, 1:-1] - moving[0][:-2, 1:-1] + (moving[1][1:-1, 2:] - moving[1][1:-1, :-2])
    )
    return 0.5 * (total + (column[..., 2:] - column[..., :-2]))


def gradient(field):
    column = pad_depth(field[1:-1, 1:-1])
    along_x = 0.5 * (field[2:, 1:-1] - field[:-2, 1:-1])
    along_y = 0.5 * (field[1:-1, 2:] - field[1:-1, :-2])
    along_z = 0.5 * (column[..., 2:] - column[..., :-2])
    return jnp.stack([along_x, along_y, along_z], 0)


def restrict(field):
    cells_x, cells_y, cells_z = field.shape
    return field.reshape(cells_x // 2, 2, cells_y // 2, 2, cells_z // 2, 2).mean(axis=(1, 3, 5))


def prolong(field):
    cells_x, cells_y, cells_z = field.shape
    spread = jnp.broadcast_to(
        field[:, None, :, None, :, None], (cells_x, 2, cells_y, 2, cells_z, 2)
    )
    return spread.reshape(2 * cells_x, 2 * cells_y, 2 * cells_z)


def advect(amounts, moving):
    flow_x = 0.5 * (moving[0][:-1, 1:-1] + moving[0][1:, 1:-1])
    flux_x = (
        jnp.maximum(flow_x, 0.0) * amounts[:, :-1, 1:-1]
        + jnp.minimum(flow_x, 0.0) * amounts[:, 1:, 1:-1]
    )
    flow_y = 0.5 * (moving[1][1:-1, :-1] + moving[1][1:-1, 1:])
    flux_y = (
        jnp.maximum(flow_y, 0.0) * amounts[:, 1:-1, :-1]
        + jnp.minimum(flow_y, 0.0) * amounts[:, 1:-1, 1:]
    )
    column = pad_depth(moving[2][1:-1, 1:-1])
    flow_z = 0.5 * (column[..., :-1] + column[..., 1:])
    center = amounts[:, 1:-1, 1:-1]
    stacked = jnp.pad(center, ((0, 0), (0, 0), (0, 0), (1, 1)))
    flux_z = (
        jnp.maximum(flow_z, 0.0) * stacked[..., :-1] + jnp.minimum(flow_z, 0.0) * stacked[..., 1:]
    )
    change = (
        flux_x[:, 1:]
        - flux_x[:, :-1]
        + (flux_y[:, :, 1:] - flux_y[:, :, :-1])
        + (flux_z[..., 1:] - flux_z[..., :-1])
    )
    return center - time_step * change


def trim_rim(field, offset):
    if offset == 0:
        return field
    return field[offset:-offset, offset:-offset]


def extend(field, width):
    return with_halo(field, (("slab", 0), ("cross", 1)), width)


def local(velocity, density, source, species):
    cells_x, cells_y, cells_z = density.shape
    halo_depth = 2
    reach = halo_depth - 1
    mobility = 1.0 / density
    bundle = jnp.concatenate([mobility[None], source[None], velocity, species], 0)
    grown = with_halo(bundle, (("slab", 1), ("cross", 2)), halo_depth)
    mobile_grown = grown[0]
    weights = face_weights(mobile_grown)
    target = divergence(grown[2:5]) - grown[1][1:-1, 1:-1]
    slab_cells = lax.axis_index("slab") * cells_x + jnp.arange(cells_x + 2) - 1
    cross_cells = lax.axis_index("cross") * cells_y + jnp.arange(cells_y + 2) - 1
    inside_x = ((slab_cells >= 0) & (slab_cells < cells_x * lax.axis_size("slab"))).astype(
        jnp.float32
    )
    inside_y = ((cross_cells >= 0) & (cross_cells < cells_y * lax.axis_size("cross"))).astype(
        jnp.float32
    )
    inside = inside_x[:, None, None] * inside_y[None, :, None]

    def sweep_once(field, extent):
        offset = reach - extent
        local_weights = tuple((trim_rim(part, offset) for part in weights))
        result = jacobi_step(field, trim_rim(target, offset), local_weights)
        if extent > 0:
            result = result * inside
        return result

    def smooth(pressure):
        pressure = sweep_once(sweep_once(extend(pressure, 2), 1), 0)
        return pressure

    fine_weights = tuple((trim_rim(part, reach) for part in weights))
    fine_target = trim_rim(target, reach)
    coarse_mobility = restrict(mobility)

    def coarse_extend(field):
        return with_halo(field, (("slab", 0), ("cross", 1)), 1)

    coarse_weights = tuple((0.25 * part for part in face_weights(coarse_extend(coarse_mobility))))
    pressure = jnp.zeros_like(density)
    for cycle_index in range(CYCLES):
        pressure = smooth(pressure)
        residual = fine_target - operate(extend(pressure, 1), fine_weights)
        coarse_target = restrict(residual)
        correction = jnp.zeros_like(coarse_target)
        for sweep_index in range(COARSE):
            correction = jacobi_step(coarse_extend(correction), coarse_target, coarse_weights)
        pressure = pressure + prolong(correction)
        pressure = smooth(pressure)
    offset = halo_depth - 1
    mobile_rim = trim_rim(mobile_grown, offset)
    velocity_rim = grown[2:5][:, offset : grown.shape[1] - offset, offset : grown.shape[2] - offset]
    species_rim = grown[5:][:, offset : grown.shape[1] - offset, offset : grown.shape[2] - offset]
    moved = (velocity_rim - mobile_rim[None] * gradient(extend(pressure, 2))) * inside[None]
    species_out = advect(species_rim, moved)
    return (moved[:, 1:-1, 1:-1], pressure, species_out)


def solution(mesh):
    return jax.shard_map(
        local,
        mesh=mesh,
        in_specs=(
            P(None, "slab", "cross", None),
            P("slab", "cross", None),
            P("slab", "cross", None),
            P(None, "slab", "cross", None),
        ),
        out_specs=(
            P(None, "slab", "cross", None),
            P("slab", "cross", None),
            P(None, "slab", "cross", None),
        ),
        check_vma=False,
    )
```

profile of v0, /device:TPU:0, one launch (start us, length us, event | category | flops | bytes accessed | tf_op | source)
XLA Modules:
  0.0 266.8 jit_solution(15936730153965526879)
XLA Ops:
  8.3 5.8 %collective-permute-start = (f32[14,2,16,128]{3,2,1,0:T(8,128)}, f32[14,2,16,128]{3,2,1,0:T(8,128)S(1)}, u32[]{:S(2)}, u32[]{:S(2)}) collective-permute-start(f32[14,2,16,128]{3,2,1,0:T(8,128)} %get-tuple-element.15), channel_id=1, source_target_pairs={{0,4},{4,8},{8,12},{12,16},{16,20},{20,24},{24,28},{1,5},{5,9},{9,... | collective-permute-start | bytes 688136 | tf_op jit(solution)/shard_map/ppermute | solution.py:19
  18.5 4.2 %collective-permute-start.8 = (f32[1,8,64]{2,1,0:T(8,128)S(1)}, f32[1,8,64]{2,1,0:T(8,128)S(1)}, u32[]{:S(2)}, u32[]{:S(2)}) collective-permute-start(f32[1,8,64]{2,1,0:T(8,128)S(1)} %get-tuple-element.90), channel_id=1, source_target_pairs={{0,4},{4,8},{8,12},{12,16},{16,20},{20,24},{24,28},{1,5},{5,9},{9,... | collective-permute-start | bytes 6152 | tf_op jit(solution)/shard_map/ppermute | solution.py:19
  24.7 4.3 %collective-permute-start.4 = (f32[2,16,128]{2,1,0:T(8,128)S(1)}, f32[2,16,128]{2,1,0:T(8,128)S(1)}, u32[]{:S(2)}, u32[]{:S(2)}) collective-permute-start(f32[2,16,128]{2,1,0:T(8,128)S(1)} %broadcast.191), channel_id=1, source_target_pairs={{0,4},{4,8},{8,12},{12,16},{16,20},{20,24},{24,28},{1,5},{5,9},{9,... | collective-permute-start | bytes 49160 | tf_op jit(solution)/shard_map/ppermute | solution.py:19
  30.3 5.1 %collective-permute-start.15 = (f32[4,1,64]{2,1,0:T(1,128)}, f32[4,1,64]{2,1,0:T(1,128)}, u32[]{:S(2)}, u32[]{:S(2)}) collective-permute-start(f32[4,1,64]{2,1,0:T(1,128)} %get-tuple-element.73), channel_id=1, source_target_pairs={{0,1},{1,2},{2,3},{4,5},{5,6},{6,7},{8,9},{9,10},{10,11},{12,13},{... | collective-permute-start | bytes 3080 | tf_op jit(solution)/shard_map/ppermute | solution.py:19
  39.8 4.7 %collective-permute-start.2 = (f32[14,8,2,128]{3,2,1,0:T(2,128)S(1)}, f32[14,8,2,128]{3,2,1,0:T(2,128)S(1)}, u32[]{:S(2)}, u32[]{:S(2)}) collective-permute-start(f32[14,8,2,128]{3,2,1,0:T(2,128)S(1)} %get-tuple-element.13), channel_id=1, source_target_pairs={{0,1},{1,2},{2,3},{4,5},{5,6},{6,7},{8,9},{9,10},{10,11},{12,13},{... | collective-permute-start | bytes 344072 | tf_op jit(solution)/shard_map/ppermute | solution.py:19
  45.8 4.5 %collective-permute-start.12 = (f32[4,1,64]{2,1,0:T(1,128)S(1)}, f32[4,1,64]{2,1,0:T(1,128)S(1)}, u32[]{:S(2)}, u32[]{:S(2)}) collective-permute-start(f32[4,1,64]{2,1,0:T(1,128)S(1)} %get-tuple-element.74), channel_id=1, source_target_pairs={{0,1},{1,2},{2,3},{4,5},{5,6},{6,7},{8,9},{9,10},{10,11},{12,13},{... | collective-permute-start | bytes 3080 | tf_op jit(solution)/shard_map/ppermute | solution.py:19
  63.7 4.8 %collective-permute-start.19 = (f32[6,1,128]{2,1,0:T(1,128)S(1)}, f32[6,1,128]{2,1,0:T(1,128)S(1)}, u32[]{:S(2)}, u32[]{:S(2)}) collective-permute-start(f32[6,1,128]{2,1,0:T(1,128)S(1)} %get-tuple-element.39), channel_id=1, source_target_pairs={{0,1},{1,2},{2,3},{4,5},{5,6},{6,7},{8,9},{9,10},{10,11},{12,13},{... | collective-permute-start | bytes 9224 | tf_op jit(solution)/shard_map/ppermute | solution.py:19
  75.2 3.4 %collective-permute-start.21 = (f32[1,8,64]{2,1,0:T(8,128)S(1)}, f32[1,8,64]{2,1,0:T(8,128)S(1)}, u32[]{:S(2)}, u32[]{:S(2)}) collective-permute-start(f32[1,8,64]{2,1,0:T(8,128)S(1)} %get-tuple-element.86), channel_id=1, source_target_pairs={{0,4},{4,8},{8,12},{12,16},{16,20},{20,24},{24,28},{1,5},{5,9},{9,... | collective-permute-start | bytes 6152 | tf_op jit(solution)/shard_map/ppermute | solution.py:19
  84.6 4.8 %collective-permute-start.23 = (f32[4,1,64]{2,1,0:T(1,128)S(1)}, f32[4,1,64]{2,1,0:T(1,128)S(1)}, u32[]{:S(2)}, u32[]{:S(2)}) collective-permute-start(f32[4,1,64]{2,1,0:T(1,128)S(1)} %get-tuple-element.69), channel_id=1, source_target_pairs={{0,1},{1,2},{2,3},{4,5},{5,6},{6,7},{8,9},{9,10},{10,11},{12,13},{... | collective-permute-start | bytes 3080 | tf_op jit(solution)/shard_map/ppermute | solution.py:19
  99.1 4.8 %collective-permute-start.27 = (f32[4,1,64]{2,1,0:T(1,128)S(1)}, f32[4,1,64]{2,1,0:T(1,128)S(1)}, u32[]{:S(2)}, u32[]{:S(2)}) collective-permute-start(f32[4,1,64]{2,1,0:T(1,128)S(1)} %get-tuple-element.67), channel_id=1, source_target_pairs={{0,1},{1,2},{2,3},{4,5},{5,6},{6,7},{8,9},{9,10},{10,11},{12,13},{... | collective-permute-start | bytes 3080 | tf_op jit(solution)/shard_map/ppermute | solution.py:19
  105.3 3.8 %collective-permute-start.29 = (f32[1,8,64]{2,1,0:T(8,128)S(1)}, f32[1,8,64]{2,1,0:T(8,128)S(1)}, u32[]{:S(2)}, u32[]{:S(2)}) collective-permute-start(f32[1,8,64]{2,1,0:T(8,128)S(1)} %get-tuple-element.82), channel_id=1, source_target_pairs={{0,4},{4,8},{8,12},{12,16},{16,20},{20,24},{24,28},{1,5},{5,9},{9,... | collective-permute-start | bytes 6152 | tf_op jit(solution)/shard_map/ppermute | solution.py:19
  114.4 4.8 %collective-permute-start.31 = (f32[4,1,64]{2,1,0:T(1,128)S(1)}, f32[4,1,64]{2,1,0:T(1,128)S(1)}, u32[]{:S(2)}, u32[]{:S(2)}) collective-permute-start(f32[4,1,64]{2,1,0:T(1,128)S(1)} %get-tuple-element.65), channel_id=1, source_target_pairs={{0,1},{1,2},{2,3},{4,5},{5,6},{6,7},{8,9},{9,10},{10,11},{12,13},{... | collective-permute-start | bytes 3080 | tf_op jit(solution)/shard_map/ppermute | solution.py:19
  123.6 3.8 %collective-permute-start.32 = (f32[2,16,128]{2,1,0:T(8,128)S(1)}, f32[2,16,128]{2,1,0:T(8,128)S(1)}, u32[]{:S(2)}, u32[]{:S(2)}) collective-permute-start(f32[2,16,128]{2,1,0:T(8,128)S(1)} %get-tuple-element.50), channel_id=1, source_target_pairs={{0,4},{4,8},{8,12},{12,16},{16,20},{20,24},{24,28},{1,5},{5,9},{9,... | collective-permute-start | bytes 49160 | tf_op jit(solution)/shard_map/ppermute | solution.py:19
  131.4 4.2 %collective-permute-start.34 = (f32[8,2,128]{2,1,0:T(2,128)S(1)}, f32[8,2,128]{2,1,0:T(2,128)S(1)}, u32[]{:S(2)}, u32[]{:S(2)}) collective-permute-start(f32[8,2,128]{2,1,0:T(2,128)S(1)} %get-tuple-element.32), channel_id=1, source_target_pairs={{0,1},{1,2},{2,3},{4,5},{5,6},{6,7},{8,9},{9,10},{10,11},{12,13},{... | collective-permute-start | bytes 24584 | tf_op jit(solution)/shard_map/ppermute | solution.py:19
  136.9 4.2 %collective-permute-done.35 = f32[8,2,128]{2,1,0:T(2,128)S(1)} collective-permute-done((f32[8,2,128]{2,1,0:T(2,128)S(1)}, f32[8,2,128]{2,1,0:T(2,128)S(1)}, u32[]{:S(2)}, u32[]{:S(2)}) %collective-permute-start.35) | collective-permute-done | bytes 8224 | tf_op jit(solution)/shard_map/ppermute | solution.py:22
  141.5 3.6 %collective-permute-start.36 = (f32[2,16,128]{2,1,0:T(8,128)S(1)}, f32[2,16,128]{2,1,0:T(8,128)S(1)}, u32[]{:S(2)}, u32[]{:S(2)}) collective-permute-start(f32[2,16,128]{2,1,0:T(8,128)S(1)} %get-tuple-element.48), channel_id=1, source_target_pairs={{0,4},{4,8},{8,12},{12,16},{16,20},{20,24},{24,28},{1,5},{5,9},{9,... | collective-permute-start | bytes 49160 | tf_op jit(solution)/shard_map/ppermute | solution.py:19
  149.3 3.9 %collective-permute-start.38 = (f32[8,2,128]{2,1,0:T(2,128)S(1)}, f32[8,2,128]{2,1,0:T(2,128)S(1)}, u32[]{:S(2)}, u32[]{:S(2)}) collective-permute-start(f32[8,2,128]{2,1,0:T(2,128)S(1)} %get-tuple-element.30), channel_id=1, source_target_pairs={{0,1},{1,2},{2,3},{4,5},{5,6},{6,7},{8,9},{9,10},{10,11},{12,13},{... | collective-permute-start | bytes 24584 | tf_op jit(solution)/shard_map/ppermute | solution.py:19
  154.5 4.2 %collective-permute-done.39 = f32[8,2,128]{2,1,0:T(2,128)S(1)} collective-permute-done((f32[8,2,128]{2,1,0:T(2,128)S(1)}, f32[8,2,128]{2,1,0:T(2,128)S(1)}, u32[]{:S(2)}, u32[]{:S(2)}) %collective-permute-start.39) | collective-permute-done | bytes 8224 | tf_op jit(solution)/shard_map/ppermute | solution.py:22
  159.1 3.4 %collective-permute-start.41 = (f32[1,16,128]{2,1,0:T(8,128)S(1)}, f32[1,16,128]{2,1,0:T(8,128)S(1)}, u32[]{:S(2)}, u32[]{:S(2)}) collective-permute-start(f32[1,16,128]{2,1,0:T(8,128)S(1)} %get-tuple-element.46), channel_id=1, source_target_pairs={{0,4},{4,8},{8,12},{12,16},{16,20},{20,24},{24,28},{1,5},{5,9},{9,... | collective-permute-start | bytes 24584 | tf_op jit(solution)/shard_map/ppermute | solution.py:19
  168.3 4.5 %collective-permute-start.43 = (f32[6,1,128]{2,1,0:T(1,128)S(1)}, f32[6,1,128]{2,1,0:T(1,128)S(1)}, u32[]{:S(2)}, u32[]{:S(2)}) collective-permute-start(f32[6,1,128]{2,1,0:T(1,128)S(1)} %get-tuple-element.37), channel_id=1, source_target_pairs={{0,1},{1,2},{2,3},{4,5},{5,6},{6,7},{8,9},{9,10},{10,11},{12,13},{... | collective-permute-start | bytes 9224 | tf_op jit(solution)/shard_map/ppermute | solution.py:19
  178.6 3.7 %collective-permute-start.45 = (f32[1,8,64]{2,1,0:T(8,128)S(1)}, f32[1,8,64]{2,1,0:T(8,128)S(1)}, u32[]{:S(2)}, u32[]{:S(2)}) collective-permute-start(f32[1,8,64]{2,1,0:T(8,128)S(1)} %get-tuple-element.80), channel_id=1, source_target_pairs={{0,4},{4,8},{8,12},{12,16},{16,20},{20,24},{24,28},{1,5},{5,9},{9,... | collective-permute-start | bytes 6152 | tf_op jit(solution)/shard_map/ppermute | solution.py:19
  187.8 4.8 %collective-permute-start.47 = (f32[4,1,64]{2,1,0:T(1,128)S(1)}, f32[4,1,64]{2,1,0:T(1,128)S(1)}, u32[]{:S(2)}, u32[]{:S(2)}) collective-permute-start(f32[4,1,64]{2,1,0:T(1,128)S(1)} %get-tuple-element.63), channel_id=1, source_target_pairs={{0,1},{1,2},{2,3},{4,5},{5,6},{6,7},{8,9},{9,10},{10,11},{12,13},{... | collective-permute-start | bytes 3080 | tf_op jit(solution)/shard_map/ppermute | solution.py:19
  194.0 3.8 %collective-permute-start.49 = (f32[1,8,64]{2,1,0:T(8,128)S(1)}, f32[1,8,64]{2,1,0:T(8,128)S(1)}, u32[]{:S(2)}, u32[]{:S(2)}) collective-permute-start(f32[1,8,64]{2,1,0:T(8,128)S(1)} %get-tuple-element.78), channel_id=1, source_target_pairs={{0,4},{4,8},{8,12},{12,16},{16,20},{20,24},{24,28},{1,5},{5,9},{9,... | collective-permute-start | bytes 6152 | tf_op jit(solution)/shard_map/ppermute | solution.py:19
  203.1 4.8 %collective-permute-start.51 = (f32[4,1,64]{2,1,0:T(1,128)S(1)}, f32[4,1,64]{2,1,0:T(1,128)S(1)}, u32[]{:S(2)}, u32[]{:S(2)}) collective-permute-start(f32[4,1,64]{2,1,0:T(1,128)S(1)} %get-tuple-element.61), channel_id=1, source_target_pairs={{0,1},{1,2},{2,3},{4,5},{5,6},{6,7},{8,9},{9,10},{10,11},{12,13},{... | collective-permute-start | bytes 3080 | tf_op jit(solution)/shard_map/ppermute | solution.py:19
  209.3 3.8 %collective-permute-start.53 = (f32[1,8,64]{2,1,0:T(8,128)S(1)}, f32[1,8,64]{2,1,0:T(8,128)S(1)}, u32[]{:S(2)}, u32[]{:S(2)}) collective-permute-start(f32[1,8,64]{2,1,0:T(8,128)S(1)} %get-tuple-element.76), channel_id=1, source_target_pairs={{0,4},{4,8},{8,12},{12,16},{16,20},{20,24},{24,28},{1,5},{5,9},{9,... | collective-permute-start | bytes 6152 | tf_op jit(solution)/shard_map/ppermute | solution.py:19
  218.4 5.0 %collective-permute-start.55 = (f32[4,1,64]{2,1,0:T(1,128)S(1)}, f32[4,1,64]{2,1,0:T(1,128)S(1)}, u32[]{:S(2)}, u32[]{:S(2)}) collective-permute-start(f32[4,1,64]{2,1,0:T(1,128)S(1)} %get-tuple-element.59), channel_id=1, source_target_pairs={{0,1},{1,2},{2,3},{4,5},{5,6},{6,7},{8,9},{9,10},{10,11},{12,13},{... | collective-permute-start | bytes 3080 | tf_op jit(solution)/shard_map/ppermute | solution.py:19
  227.5 3.8 %collective-permute-start.56 = (f32[2,16,128]{2,1,0:T(8,128)S(1)}, f32[2,16,128]{2,1,0:T(8,128)S(1)}, u32[]{:S(2)}, u32[]{:S(2)}) collective-permute-start(f32[2,16,128]{2,1,0:T(8,128)S(1)} %get-tuple-element.44), channel_id=1, source_target_pairs={{0,4},{4,8},{8,12},{12,16},{16,20},{20,24},{24,28},{1,5},{5,9},{9,... | collective-permute-start | bytes 49160 | tf_op jit(solution)/shard_map/ppermute | solution.py:19
  235.3 4.2 %collective-permute-start.58 = (f32[8,2,128]{2,1,0:T(2,128)S(1)}, f32[8,2,128]{2,1,0:T(2,128)S(1)}, u32[]{:S(2)}, u32[]{:S(2)}) collective-permute-start(f32[8,2,128]{2,1,0:T(2,128)S(1)} %get-tuple-element.28), channel_id=1, source_target_pairs={{0,1},{1,2},{2,3},{4,5},{5,6},{6,7},{8,9},{9,10},{10,11},{12,13},{... | collective-permute-start | bytes 24584 | tf_op jit(solution)/shard_map/ppermute | solution.py:19
  240.8 4.2 %collective-permute-done.59 = f32[8,2,128]{2,1,0:T(2,128)S(1)} collective-permute-done((f32[8,2,128]{2,1,0:T(2,128)S(1)}, f32[8,2,128]{2,1,0:T(2,128)S(1)}, u32[]{:S(2)}, u32[]{:S(2)}) %collective-permute-start.59) | collective-permute-done | bytes 8224 | tf_op jit(solution)/shard_map/ppermute | solution.py:22
  246.2 3.6 %collective-permute-start.60 = (f32[2,16,128]{2,1,0:T(8,128)S(1)}, f32[2,16,128]{2,1,0:T(8,128)S(1)}, u32[]{:S(2)}, u32[]{:S(2)}) collective-permute-start(f32[2,16,128]{2,1,0:T(8,128)S(1)} %get-tuple-element.42), channel_id=1, source_target_pairs={{0,4},{4,8},{8,12},{12,16},{16,20},{20,24},{24,28},{1,5},{5,9},{9,... | collective-permute-start | bytes 49160 | tf_op jit(solution)/shard_map/ppermute | solution.py:19
  254.0 3.9 %collective-permute-start.62 = (f32[8,2,128]{2,1,0:T(2,128)S(1)}, f32[8,2,128]{2,1,0:T(2,128)S(1)}, u32[]{:S(2)}, u32[]{:S(2)}) collective-permute-start(f32[8,2,128]{2,1,0:T(2,128)S(1)} %get-tuple-element.26), channel_id=1, source_target_pairs={{0,1},{1,2},{2,3},{4,5},{5,6},{6,7},{8,9},{9,10},{10,11},{12,13},{... | collective-permute-start | bytes 24584 | tf_op jit(solution)/shard_map/ppermute | solution.py:19
  259.3 4.2 %collective-permute-done.63 = f32[8,2,128]{2,1,0:T(2,128)S(1)} collective-permute-done((f32[8,2,128]{2,1,0:T(2,128)S(1)}, f32[8,2,128]{2,1,0:T(2,128)S(1)}, u32[]{:S(2)}, u32[]{:S(2)}) %collective-permute-start.63) | collective-permute-done | bytes 8224 | tf_op jit(solution)/shard_map/ppermute | solution.py:22
  (237 shorter events, 127.9 us)
Async XLA Ops:
  0.6 17.8 %collective-permute-start.11 = (f32[1,8,64]{2,1,0:T(8,128)S(1)}, f32[1,8,64]{2,1,0:T(8,128)S(1)}, u32[]{:S(2)}, u32[]{:S(2)}) collective-permute-start(f32[1,8,64]{2,1,0:T(8,128)S(1)} %broadcast.202), channel_id=1, source_target_pairs={{0,4},{4,8},{8,12},{12,16},{16,20},{20,24},{24,28},{1,5},{5,9},{9,... | collective-permute-start | bytes 6152 | tf_op jit(solution)/shard_map/ppermute | solution.py:19
  3.0 19.7 %collective-permute-start.10 = (f32[1,8,64]{2,1,0:T(8,128)S(1)}, f32[1,8,64]{2,1,0:T(8,128)S(1)}, u32[]{:S(2)}, u32[]{:S(2)}) collective-permute-start(f32[1,8,64]{2,1,0:T(8,128)S(1)} %broadcast.202), channel_id=1, source_target_pairs={{4,0},{8,4},{12,8},{16,12},{20,16},{24,20},{28,24},{5,1},{9,5},{13... | collective-permute-start | bytes 6152 | tf_op jit(solution)/shard_map/ppermute | solution.py:22
  4.4 25.9 %collective-permute-start.5 = (f32[2,16,128]{2,1,0:T(8,128)S(1)}, f32[2,16,128]{2,1,0:T(8,128)S(1)}, u32[]{:S(2)}, u32[]{:S(2)}) collective-permute-start(f32[2,16,128]{2,1,0:T(8,128)S(1)} %broadcast.191), channel_id=1, source_target_pairs={{4,0},{8,4},{12,8},{16,12},{20,16},{24,20},{28,24},{5,1},{9,5},{13... | collective-permute-start | bytes 49160 | tf_op jit(solution)/shard_map/ppermute | solution.py:22
  8.3 30.1 %collective-permute-start = (f32[14,2,16,128]{3,2,1,0:T(8,128)}, f32[14,2,16,128]{3,2,1,0:T(8,128)S(1)}, u32[]{:S(2)}, u32[]{:S(2)}) collective-permute-start(f32[14,2,16,128]{3,2,1,0:T(8,128)} %get-tuple-element.15), channel_id=1, source_target_pairs={{0,4},{4,8},{8,12},{12,16},{16,20},{20,24},{24,28},{1,5},{5,9},{9,... | collective-permute-start | bytes 688136 | tf_op jit(solution)/shard_map/ppermute | solution.py:19
  14.0 25.7 %collective-permute-start.1 = (f32[14,2,16,128]{3,2,1,0:T(8,128)}, f32[14,2,16,128]{3,2,1,0:T(8,128)S(1)}, u32[]{:S(2)}, u32[]{:S(2)}) collective-permute-start(f32[14,2,16,128]{3,2,1,0:T(8,128)} %get-tuple-element.16), channel_id=1, source_target_pairs={{4,0},{8,4},{12,8},{16,12},{20,16},{24,20},{28,24},{5,1},{9,5},{13... | collective-permute-start | bytes 688136 | tf_op jit(solution)/shard_map/ppermute | solution.py:22
  18.5 6.2 %collective-permute-start.8 = (f32[1,8,64]{2,1,0:T(8,128)S(1)}, f32[1,8,64]{2,1,0:T(8,128)S(1)}, u32[]{:S(2)}, u32[]{:S(2)}) collective-permute-start(f32[1,8,64]{2,1,0:T(8,128)S(1)} %get-tuple-element.90), channel_id=1, source_target_pairs={{0,4},{4,8},{8,12},{12,16},{16,20},{20,24},{24,28},{1,5},{5,9},{9,... | collective-permute-start | bytes 6152 | tf_op jit(solution)/shard_map/ppermute | solution.py:19
  22.7 6.2 %collective-permute-start.9 = (f32[1,8,64]{2,1,0:T(8,128)S(1)}, f32[1,8,64]{2,1,0:T(8,128)S(1)}, u32[]{:S(2)}, u32[]{:S(2)}) collective-permute-start(f32[1,8,64]{2,1,0:T(8,128)S(1)} %get-tuple-element.91), channel_id=1, source_target_pairs={{4,0},{8,4},{12,8},{16,12},{20,16},{24,20},{28,24},{5,1},{9,5},{13... | collective-permute-start | bytes 6152 | tf_op jit(solution)/shard_map/ppermute | solution.py:22
  24.7 10.7 %collective-permute-start.4 = (f32[2,16,128]{2,1,0:T(8,128)S(1)}, f32[2,16,128]{2,1,0:T(8,128)S(1)}, u32[]{:S(2)}, u32[]{:S(2)}) collective-permute-start(f32[2,16,128]{2,1,0:T(8,128)S(1)} %broadcast.191), channel_id=1, source_target_pairs={{0,4},{4,8},{8,12},{12,16},{16,20},{20,24},{24,28},{1,5},{5,9},{9,... | collective-permute-start | bytes 49160 | tf_op jit(solution)/shard_map/ppermute | solution.py:19
  28.9 44.6 %collective-permute-start.14 = (f32[4,1,64]{2,1,0:T(1,128)}, f32[4,1,64]{2,1,0:T(1,128)}, u32[]{:S(2)}, u32[]{:S(2)}) collective-permute-start(f32[4,1,64]{2,1,0:T(1,128)} %get-tuple-element.72), channel_id=1, source_target_pairs={{1,0},{2,1},{3,2},{5,4},{6,5},{7,6},{9,8},{10,9},{11,10},{13,12},{... | collective-permute-start | bytes 3080 | tf_op jit(solution)/shard_map/ppermute | solution.py:22
  30.3 43.3 %collective-permute-start.15 = (f32[4,1,64]{2,1,0:T(1,128)}, f32[4,1,64]{2,1,0:T(1,128)}, u32[]{:S(2)}, u32[]{:S(2)}) collective-permute-start(f32[4,1,64]{2,1,0:T(1,128)} %get-tuple-element.73), channel_id=1, source_target_pairs={{0,1},{1,2},{2,3},{4,5},{5,6},{6,7},{8,9},{9,10},{10,11},{12,13},{... | collective-permute-start | bytes 3080 | tf_op jit(solution)/shard_map/ppermute | solution.py:19
  35.4 9.1 %collective-permute-start.6 = (f32[8,2,128]{2,1,0:T(2,128)S(1)}, f32[8,2,128]{2,1,0:T(2,128)S(1)}, u32[]{:S(2)}, u32[]{:S(2)}) collective-permute-start(f32[8,2,128]{2,1,0:T(2,128)S(1)} %get-tuple-element.34), channel_id=1, source_target_pairs={{0,1},{1,2},{2,3},{4,5},{5,6},{6,7},{8,9},{9,10},{10,11},{12,13},{... | collective-permute-start | bytes 24584 | tf_op jit(solution)/shard_map/ppermute | solution.py:19
  38.4 7.4 %collective-permute-start.7 = (f32[8,2,128]{2,1,0:T(2,128)S(1)}, f32[8,2,128]{2,1,0:T(2,128)S(1)}, u32[]{:S(2)}, u32[]{:S(2)}) collective-permute-start(f32[8,2,128]{2,1,0:T(2,128)S(1)} %get-tuple-element.35), channel_id=1, source_target_pairs={{1,0},{2,1},{3,2},{5,4},{6,5},{7,6},{9,8},{10,9},{11,10},{13,12},{... | collective-permute-start | bytes 24584 | tf_op jit(solution)/shard_map/ppermute | solution.py:22
  39.8 10.6 %collective-permute-start.2 = (f32[14,8,2,128]{3,2,1,0:T(2,128)S(1)}, f32[14,8,2,128]{3,2,1,0:T(2,128)S(1)}, u32[]{:S(2)}, u32[]{:S(2)}) collective-permute-start(f32[14,8,2,128]{3,2,1,0:T(2,128)S(1)} %get-tuple-element.13), channel_id=1, source_target_pairs={{0,1},{1,2},{2,3},{4,5},{5,6},{6,7},{8,9},{9,10},{10,11},{12,13},{... | collective-permute-start | bytes 344072 | tf_op jit(solution)/shard_map/ppermute | solution.py:19
  44.5 7.6 %collective-permute-start.3 = (f32[14,8,2,128]{3,2,1,0:T(2,128)S(1)}, f32[14,8,2,128]{3,2,1,0:T(2,128)S(1)}, u32[]{:S(2)}, u32[]{:S(2)}) collective-permute-start(f32[14,8,2,128]{3,2,1,0:T(2,128)S(1)} %get-tuple-element.14), channel_id=1, source_target_pairs={{1,0},{2,1},{3,2},{5,4},{6,5},{7,6},{9,8},{10,9},{11,10},{13,12},{... | collective-permute-start | bytes 344072 | tf_op jit(solution)/shard_map/ppermute | solution.py:22
  45.8 17.8 %collective-permute-start.12 = (f32[4,1,64]{2,1,0:T(1,128)S(1)}, f32[4,1,64]{2,1,0:T(1,128)S(1)}, u32[]{:S(2)}, u32[]{:S(2)}) collective-permute-start(f32[4,1,64]{2,1,0:T(1,128)S(1)} %get-tuple-element.74), channel_id=1, source_target_pairs={{0,1},{1,2},{2,3},{4,5},{5,6},{6,7},{8,9},{9,10},{10,11},{12,13},{... | collective-permute-start | bytes 3080 | tf_op jit(solution)/shard_map/ppermute | solution.py:19
  56.3 6.0 %collective-permute-start.16 = (f32[1,16,128]{2,1,0:T(8,128)S(1)}, f32[1,16,128]{2,1,0:T(8,128)S(1)}, u32[]{:S(2)}, u32[]{:S(2)}) collective-permute-start(f32[1,16,128]{2,1,0:T(8,128)S(1)} %get-tuple-element.55), channel_id=1, source_target_pairs={{4,0},{8,4},{12,8},{16,12},{20,16},{24,20},{28,24},{5,1},{9,5},{13... | collective-permute-start | bytes 24584 | tf_op jit(solution)/shard_map/ppermute | solution.py:22
  58.2 10.3 %collective-permute-start.13 = (f32[4,1,64]{2,1,0:T(1,128)S(1)}, f32[4,1,64]{2,1,0:T(1,128)S(1)}, u32[]{:S(2)}, u32[]{:S(2)}) collective-permute-start(f32[4,1,64]{2,1,0:T(1,128)S(1)} %get-tuple-element.75), channel_id=1, source_target_pairs={{1,0},{2,1},{3,2},{5,4},{6,5},{7,6},{9,8},{10,9},{11,10},{13,12},{... | collective-permute-start | bytes 3080 | tf_op jit(solution)/shard_map/ppermute | solution.py:22
  62.4 6.8 %collective-permute-start.18 = (f32[6,1,128]{2,1,0:T(1,128)S(1)}, f32[6,1,128]{2,1,0:T(1,128)S(1)}, u32[]{:S(2)}, u32[]{:S(2)}) collective-permute-start(f32[6,1,128]{2,1,0:T(1,128)S(1)} %get-tuple-element.38), channel_id=1, source_target_pairs={{1,0},{2,1},{3,2},{5,4},{6,5},{7,6},{9,8},{10,9},{11,10},{13,12},{... | collective-permute-start | bytes 9224 | tf_op jit(solution)/shard_map/ppermute | solution.py:22
  63.7 6.1 %collective-permute-start.19 = (f32[6,1,128]{2,1,0:T(1,128)S(1)}, f32[6,1,128]{2,1,0:T(1,128)S(1)}, u32[]{:S(2)}, u32[]{:S(2)}) collective-permute-start(f32[6,1,128]{2,1,0:T(1,128)S(1)} %get-tuple-element.39), channel_id=1, source_target_pairs={{0,1},{1,2},{2,3},{4,5},{5,6},{6,7},{8,9},{9,10},{10,11},{12,13},{... | collective-permute-start | bytes 9224 | tf_op jit(solution)/shard_map/ppermute | solution.py:19
  83.3 6.1 %collective-permute-start.22 = (f32[4,1,64]{2,1,0:T(1,128)S(1)}, f32[4,1,64]{2,1,0:T(1,128)S(1)}, u32[]{:S(2)}, u32[]{:S(2)}) collective-permute-start(f32[4,1,64]{2,1,0:T(1,128)S(1)} %get-tuple-element.68), channel_id=1, source_target_pairs={{1,0},{2,1},{3,2},{5,4},{6,5},{7,6},{9,8},{10,9},{11,10},{13,12},{... | collective-permute-start | bytes 3080 | tf_op jit(solution)/shard_map/ppermute | solution.py:22
  84.6 6.1 %collective-permute-start.23 = (f32[4,1,64]{2,1,0:T(1,128)S(1)}, f32[4,1,64]{2,1,0:T(1,128)S(1)}, u32[]{:S(2)}, u32[]{:S(2)}) collective-permute-start(f32[4,1,64]{2,1,0:T(1,128)S(1)} %get-tuple-element.69), channel_id=1, source_target_pairs={{0,1},{1,2},{2,3},{4,5},{5,6},{6,7},{8,9},{9,10},{10,11},{12,13},{... | collective-permute-start | bytes 3080 | tf_op jit(solution)/shard_map/ppermute | solution.py:19
  97.8 6.1 %collective-permute-start.26 = (f32[4,1,64]{2,1,0:T(1,128)S(1)}, f32[4,1,64]{2,1,0:T(1,128)S(1)}, u32[]{:S(2)}, u32[]{:S(2)}) collective-permute-start(f32[4,1,64]{2,1,0:T(1,128)S(1)} %get-tuple-element.66), channel_id=1, source_target_pairs={{1,0},{2,1},{3,2},{5,4},{6,5},{7,6},{9,8},{10,9},{11,10},{13,12},{... | collective-permute-start | bytes 3080 | tf_op jit(solution)/shard_map/ppermute | solution.py:22
  99.1 6.1 %collective-permute-start.27 = (f32[4,1,64]{2,1,0:T(1,128)S(1)}, f32[4,1,64]{2,1,0:T(1,128)S(1)}, u32[]{:S(2)}, u32[]{:S(2)}) collective-permute-start(f32[4,1,64]{2,1,0:T(1,128)S(1)} %get-tuple-element.67), channel_id=1, source_target_pairs={{0,1},{1,2},{2,3},{4,5},{5,6},{6,7},{8,9},{9,10},{10,11},{12,13},{... | collective-permute-start | bytes 3080 | tf_op jit(solution)/shard_map/ppermute | solution.py:19
  113.1 6.1 %collective-permute-start.30 = (f32[4,1,64]{2,1,0:T(1,128)S(1)}, f32[4,1,64]{2,1,0:T(1,128)S(1)}, u32[]{:S(2)}, u32[]{:S(2)}) collective-permute-start(f32[4,1,64]{2,1,0:T(1,128)S(1)} %get-tuple-element.64), channel_id=1, source_target_pairs={{1,0},{2,1},{3,2},{5,4},{6,5},{7,6},{9,8},{10,9},{11,10},{13,12},{... | collective-permute-start | bytes 3080 | tf_op jit(solution)/shard_map/ppermute | solution.py:22
  114.4 6.1 %collective-permute-start.31 = (f32[4,1,64]{2,1,0:T(1,128)S(1)}, f32[4,1,64]{2,1,0:T(1,128)S(1)}, u32[]{:S(2)}, u32[]{:S(2)}) collective-permute-start(f32[4,1,64]{2,1,0:T(1,128)S(1)} %get-tuple-element.65), channel_id=1, source_target_pairs={{0,1},{1,2},{2,3},{4,5},{5,6},{6,7},{8,9},{9,10},{10,11},{12,13},{... | collective-permute-start | bytes 3080 | tf_op jit(solution)/shard_map/ppermute | solution.py:19
  168.3 5.9 %collective-permute-start.43 = (f32[6,1,128]{2,1,0:T(1,128)S(1)}, f32[6,1,128]{2,1,0:T(1,128)S(1)}, u32[]{:S(2)}, u32[]{:S(2)}) collective-permute-start(f32[6,1,128]{2,1,0:T(1,128)S(1)} %get-tuple-element.37), channel_id=1, source_target_pairs={{0,1},{1,2},{2,3},{4,5},{5,6},{6,7},{8,9},{9,10},{10,11},{12,13},{... | collective-permute-start | bytes 9224 | tf_op jit(solution)/shard_map/ppermute | solution.py:19
  186.5 6.1 %collective-permute-start.46 = (f32[4,1,64]{2,1,0:T(1,128)S(1)}, f32[4,1,64]{2,1,0:T(1,128)S(1)}, u32[]{:S(2)}, u32[]{:S(2)}) collective-permute-start(f32[4,1,64]{2,1,0:T(1,128)S(1)} %get-tuple-element.62), channel_id=1, source_target_pairs={{1,0},{2,1},{3,2},{5,4},{6,5},{7,6},{9,8},{10,9},{11,10},{13,12},{... | collective-permute-start | bytes 3080 | tf_op jit(solution)/shard_map/ppermute | solution.py:22
  187.8 6.1 %collective-permute-start.47 = (f32[4,1,64]{2,1,0:T(1,128)S(1)}, f32[4,1,64]{2,1,0:T(1,128)S(1)}, u32[]{:S(2)}, u32[]{:S(2)}) collective-permute-start(f32[4,1,64]{2,1,0:T(1,128)S(1)} %get-tuple-element.63), channel_id=1, source_target_pairs={{0,1},{1,2},{2,3},{4,5},{5,6},{6,7},{8,9},{9,10},{10,11},{12,13},{... | collective-permute-start | bytes 3080 | tf_op jit(solution)/shard_map/ppermute | solution.py:19
  201.8 6.1 %collective-permute-start.50 = (f32[4,1,64]{2,1,0:T(1,128)S(1)}, f32[4,1,64]{2,1,0:T(1,128)S(1)}, u32[]{:S(2)}, u32[]{:S(2)}) collective-permute-start(f32[4,1,64]{2,1,0:T(1,128)S(1)} %get-tuple-element.60), channel_id=1, source_target_pairs={{1,0},{2,1},{3,2},{5,4},{6,5},{7,6},{9,8},{10,9},{11,10},{13,12},{... | collective-permute-start | bytes 3080 | tf_op jit(solution)/shard_map/ppermute | solution.py:22
  203.1 6.1 %collective-permute-start.51 = (f32[4,1,64]{2,1,0:T(1,128)S(1)}, f32[4,1,64]{2,1,0:T(1,128)S(1)}, u32[]{:S(2)}, u32[]{:S(2)}) collective-permute-start(f32[4,1,64]{2,1,0:T(1,128)S(1)} %get-tuple-element.61), channel_id=1, source_target_pairs={{0,1},{1,2},{2,3},{4,5},{5,6},{6,7},{8,9},{9,10},{10,11},{12,13},{... | collective-permute-start | bytes 3080 | tf_op jit(solution)/shard_map/ppermute | solution.py:19
  217.1 6.3 %collective-permute-start.54 = (f32[4,1,64]{2,1,0:T(1,128)S(1)}, f32[4,1,64]{2,1,0:T(1,128)S(1)}, u32[]{:S(2)}, u32[]{:S(2)}) collective-permute-start(f32[4,1,64]{2,1,0:T(1,128)S(1)} %get-tuple-element.58), channel_id=1, source_target_pairs={{1,0},{2,1},{3,2},{5,4},{6,5},{7,6},{9,8},{10,9},{11,10},{13,12},{... | collective-permute-start | bytes 3080 | tf_op jit(solution)/shard_map/ppermute | solution.py:22
  218.4 6.1 %collective-permute-start.55 = (f32[4,1,64]{2,1,0:T(1,128)S(1)}, f32[4,1,64]{2,1,0:T(1,128)S(1)}, u32[]{:S(2)}, u32[]{:S(2)}) collective-permute-start(f32[4,1,64]{2,1,0:T(1,128)S(1)} %get-tuple-element.59), channel_id=1, source_target_pairs={{0,1},{1,2},{2,3},{4,5},{5,6},{6,7},{8,9},{9,10},{10,11},{12,13},{... | collective-permute-start | bytes 3080 | tf_op jit(solution)/shard_map/ppermute | solution.py:19
  (49 other events, 451.5 us)
where the time goes:
time: 272 us; the launch traced here: 267 us
  starting transfers between devices  172 us (63%)
  waiting for transfers between devices  61.6 us (23%)
  other arithmetic  16 us (6%)
  local copies, waits for them, and re-layouts  15.4 us (6%)
    ppermute x32, starting transfers between devices, with_halo(): lax.ppermute(lax.slice_in_dim(block, block.shape[dim] - width, None, axis...  131 us
    ppermute x32, waiting for transfers between devices, with_halo(): lax.ppermute(lax.slice_in_dim(block, 0, width, axis=dim), axis, backward)  51.9 us
    ppermute x32, starting transfers between devices, with_halo(): lax.ppermute(lax.slice_in_dim(block, 0, width, axis=dim), axis, backward)  41.3 us
    ppermute x32, waiting for transfers between devices, with_halo(): lax.ppermute(lax.slice_in_dim(block, block.shape[dim] - width, None, axis...  9.71 us
    reshape x3, local copies, waits for them, and re-layouts, restrict(): field.reshape(cells_x // 2, 2, cells_y // 2, 2, cells_z // 2, 2)  7.75 us
  transfers between devices with their start and end apart: 64, of which 25 were waited for; matrix products, arithmetic and copies ran while one was open for 5% of the time, Pallas kernels for 0%

commit v1 on v0

v1 whole, which is shorter than its diff:
```python
import functools

import jax
import jax.numpy as jnp
from jax import lax
from jax.experimental import pallas as pl
from jax.experimental.pallas import tpu as pltpu
from jax.sharding import PartitionSpec as P

CYCLES = 2
COARSE = 4
damping = 0.8
time_step = 0.25
MESH = pl.DeviceIdType.MESH
HX = 4
HY = 8
KY = 4

NEAR = [(dx, dy) for dx in (-1, 0, 1) for dy in (-1, 0, 1) if (dx, dy) != (0, 0)]
WIDE = [(dx, dy) for dx in (-2, -1, 0, 1, 2) for dy in (-1, 0, 1) if (dx, dy) != (0, 0)]
SIDE = [(-1, 0), (1, 0), (0, -1), (0, 1)]


def kernel(
    slabs, crosses, velocity, density, source, species, vel_out, pres_out, spec_out,
    fields, coarse_m, rhs, press, rim_x, rim_y, last,
    xa, xb, ya, yb, za, zb, goal, scale_back, pa, pb,
    cxa, cxb, cya, cyb, cza, czb, cinv, ca, cb,
    f_send, f_recv, m_send, m_recv, r_send, r_recv, p_send, p_recv, s_send, s_recv, l_send, l_recv,
):
    cells_x, cells_y, cells_z = density.shape
    wx, wy = cells_x + 2 * HX, cells_y + 2 * HY
    half = cells_x // 2
    cw = cells_x // 2 + 4 * half
    own_y = pl.ds(HY, cells_y)
    own_x = pl.ds(HX, cells_x)
    own_c = pl.ds(2 * half, half)
    slab, cross = lax.axis_index("slab"), lax.axis_index("cross")
    f32 = jnp.float32

    def there(dx, dy):
        return (slab + dx >= 0) & (slab + dx < slabs) & (cross + dy >= 0) & (cross + dy < crosses)

    def ys(dy, k):
        if dy == 0:
            return own_y, own_y
        if dy > 0:
            return pl.ds(HY + cells_y - k, k), pl.ds(HY - k, k)
        return pl.ds(HY, k), pl.ds(HY + cells_y, k)

    def fine_cut(ref, dx, dy, k, lead):
        sy, dyy = ys(dy, k)
        dst_x = pl.ds(HX - dx * cells_x, cells_x)
        pre = (slice(None),) if lead else ()
        return ref.at[pre + (own_x, sy)], ref.at[pre + (dst_x, dyy)]

    def coarse_cut(ref, dx, dy, at=None):
        sy, dyy = ys(dy, HY)
        dst_x = pl.ds(2 * half - dx * half, half)
        pre = () if at is None else (at,)
        return ref.at[pre + (own_c, sy)], ref.at[pre + (dst_x, dyy)]

    def exchange(directions, cut, send, recv):
        def copy(index, dx, dy):
            src, dst = cut(dx, dy)
            return pltpu.make_async_remote_copy(
                src_ref=src, dst_ref=dst, send_sem=send.at[index], recv_sem=recv.at[index],
                device_id=(slab + dx, cross + dy), device_id_type=MESH,
            )

        def start():
            for index, (dx, dy) in enumerate(directions):
                @pl.when(there(dx, dy))
                def _():
                    copy(index, dx, dy).start()

        def arrive():
            for index, (dx, dy) in enumerate(directions):
                @pl.when(there(-dx, -dy))
                def _():
                    copy(index, dx, dy).wait_recv()

        def leave():
            for index, (dx, dy) in enumerate(directions):
                @pl.when(there(dx, dy))
                def _():
                    copy(index, dx, dy).wait_send()

        return start, arrive, leave

    f_x = exchange(NEAR, lambda dx, dy: fine_cut(fields, dx, dy, KY, True), f_send, f_recv)
    m_x = exchange(WIDE, lambda dx, dy: coarse_cut(coarse_m, dx, dy), m_send, m_recv)
    r_x = [
        exchange(WIDE, lambda dx, dy, at=at: coarse_cut(rhs, dx, dy, at), r_send.at[at], r_recv.at[at])
        for at in range(CYCLES)
    ]
    p_x = exchange(NEAR, lambda dx, dy: fine_cut(press, dx, dy, KY, False), p_send, p_recv)

    def last_cut(dx, dy):
        if dx != 0:
            src = pl.ds(HX + cells_x - 2, 2) if dx > 0 else pl.ds(HX, 2)
            dst = pl.ds(HX - 2, 2) if dx > 0 else pl.ds(HX + cells_x, 2)
            return last.at[src, own_y], last.at[dst, own_y]
        sy, dyy = ys(dy, 2)
        return last.at[own_x, sy], last.at[own_x, dyy]

    l_x = exchange(SIDE, last_cut, l_send, l_recv)

    def species_cut(dx, dy):
        if dx != 0:
            return species.at[:, cells_x - 1 if dx > 0 else 0], rim_x.at[0 if dx > 0 else 1]
        row = cells_y - 1 if dy > 0 else 0
        return species.at[:, :, pl.ds(row, 1)], rim_y.at[0 if dy > 0 else 1, :, :, pl.ds(0, 1)]

    s_x = exchange(SIDE, species_cut, s_send, s_recv)

    def grids(rows):
        lane = lax.broadcasted_iota(jnp.int32, (rows, cells_z), 1)
        row = lax.broadcasted_iota(jnp.int32, (rows, cells_z), 0)
        return row, lane

    def next_z(v, k=1):
        return pltpu.roll(v, cells_z - k, 1)

    def prev_z(v, k=1):
        return pltpu.roll(v, k, 1)

    def next_y(v, k=1):
        return pltpu.roll(v, v.shape[0] - k, 0)

    def prev_y(v, k=1):
        return pltpu.roll(v, k, 0)

    row_w, lane_w = grids(wy)
    row_o, lane_o = grids(cells_y)

    def pair_sum(v, row, lane):
        v = v + jnp.where(row % 2 == 0, next_y(v), prev_y(v))
        return v + jnp.where(lane % 2 == 0, next_z(v), prev_z(v))

    for ref in (fields, coarse_m, rhs, press, rim_x, rim_y, last):
        ref[...] = jnp.zeros(ref.shape, f32)
    for x in range(cells_x):
        v2 = velocity[2, x]
        dz = jnp.where(lane_o == cells_z - 1, 0.0, next_z(v2)) - jnp.where(lane_o == 0, 0.0, prev_z(v2))
        fields[0, HX + x, own_y] = 1.0 / density[x]
        fields[1, HX + x, own_y] = velocity[0, x]
        fields[2, HX + x, own_y] = velocity[1, x]
        fields[3, HX + x, own_y] = 0.5 * dz - source[x]
    for c in range(half):
        m = 1.0 / density[2 * c] + 1.0 / density[2 * c + 1]
        coarse_m[2 * half + c, own_y] = 0.125 * pair_sum(m, row_o, lane_o)

    barrier = pltpu.get_barrier_semaphore()
    count = jnp.int32(0)
    for dx, dy in WIDE:
        here = there(dx, dy)
        count = count + here.astype(jnp.int32)

        @pl.when(here)
        def _():
            pl.semaphore_signal(barrier, inc=1, device_id=(slab + dx, cross + dy), device_id_type=MESH)

    pl.semaphore_wait(barrier, count)
    f_x[0]()
    m_x[0]()
    s_x[0]()
    f_x[1]()

    for x in range(1, wx - 1):
        m = fields[0, x]
        lo_x, hi_x = 0.5 * (m + fields[0, x - 1]), 0.5 * (m + fields[0, x + 1])
        lo_y, hi_y = 0.5 * (m + prev_y(m)), 0.5 * (m + next_y(m))
        lo_z = 0.5 * (m + jnp.where(lane_w == 0, 0.0, prev_z(m)))
        hi_z = 0.5 * (m + jnp.where(lane_w == cells_z - 1, 0.0, next_z(m)))
        diag = lo_x + hi_x + lo_y + hi_y + lo_z + hi_z
        inside = m > 0.0
        inv = jnp.where(inside, damping / jnp.where(inside, diag, 1.0), 0.0)
        xa[x], xb[x] = lo_x * inv, hi_x * inv
        ya[x], yb[x] = lo_y * inv, hi_y * inv
        za[x] = jnp.where(lane_w == 0, 0.0, lo_z * inv)
        zb[x] = jnp.where(lane_w == cells_z - 1, 0.0, hi_z * inv)
        if HX <= x < HX + cells_x:
            scale_back[x - HX] = (diag * (1.0 / damping))[HY : HY + cells_y]
        v1 = fields[2, x]
        t = 0.5 * ((fields[1, x + 1] - fields[1, x - 1]) + (next_y(v1) - prev_y(v1))) + fields[3, x]
        b = t * inv
        goal[x] = b
        pa[x] = -b

    def sweep(src, dst, coefs, right, low, high, k):
        xl, xu, yl, yu, zl, zu = coefs
        for x in range(low, high):
            v = src[x]
            t = xl[x] * src[x - 1] + xu[x] * src[x + 1]
            t = t + (yl[x] * prev_y(v, k) + yu[x] * next_y(v, k))
            t = t + (zl[x] * prev_z(v, k) + zu[x] * next_z(v, k))
            dst[x] = (1.0 - damping) * v + (t - right[x])

    fine = (xa, xb, ya, yb, za, zb)
    coarse = (cxa, cxb, cya, cyb, cza, czb)

    def coarse_setup():
        for x in range(1, cw - 1):
            m = coarse_m[x]
            lo_x, hi_x = 0.5 * (m + coarse_m[x - 1]), 0.5 * (m + coarse_m[x + 1])
            lo_y, hi_y = 0.5 * (m + prev_y(m, 2)), 0.5 * (m + next_y(m, 2))
            lo_z = 0.5 * (m + jnp.where(lane_w < 2, 0.0, prev_z(m, 2)))
            hi_z = 0.5 * (m + jnp.where(lane_w >= cells_z - 2, 0.0, next_z(m, 2)))
            diag = lo_x + hi_x + lo_y + hi_y + lo_z + hi_z
            inside = m > 0.0
            inv = jnp.where(inside, damping / jnp.where(inside, diag, 1.0), 0.0)
            cxa[x], cxb[x] = lo_x * inv, hi_x * inv
            cya[x], cyb[x] = lo_y * inv, hi_y * inv
            cza[x] = jnp.where(lane_w < 2, 0.0, lo_z * inv)
            czb[x] = jnp.where(lane_w >= cells_z - 2, 0.0, hi_z * inv)
            if 2 * half <= x < 3 * half:
                cinv[x - 2 * half] = inv[HY : HY + cells_y]

    def correct(at, pre):
        if at == 0:
            m_x[1]()
            coarse_setup()
        for c in range(half):
            r = None
            for x in (HX + 2 * c, HX + 2 * c + 1):
                v = pre[x]
                t = xa[x] * pre[x - 1] + xb[x] * pre[x + 1]
                t = t + (ya[x] * prev_y(v) + yb[x] * next_y(v))
                t = t + (za[x] * prev_z(v) + zb[x] * next_z(v))
                d = (damping * v - (t - goal[x]))[HY : HY + cells_y] * scale_back[x - HX]
                r = d if r is None else r + d
            rhs[at, 2 * half + c, own_y] = 0.5 * pair_sum(r, row_o, lane_o) * cinv[c]
        r_x[at][0]()
        r_x[at][1]()
        right = rhs.at[at]
        for x in range(cw):
            ca[x] = -right[x]
        src, dst = ca, cb
        for step in range(1, COARSE):
            sweep(src, dst, coarse, right, step, cw - step, 2)
            src, dst = dst, src
        other = pb if pre is pa else pa
        for x in range(2, wx - 2):
            pre[x] = pre[x] + src[2 * half + (x - HX) // 2]
        sweep(pre, other, fine, goal, 3, wx - 3, 1)
        sweep(other, pre, fine, goal, HX, HX + cells_x, 1)

    sweep(pa, pb, fine, goal, 2, wx - 2, 1)
    correct(0, pb)
    for x in range(HX, HX + cells_x):
        press[x, own_y] = pb[x, own_y]
    p_x[0]()
    p_x[1]()
    sweep(press, pa, fine, goal, 1, wx - 1, 1)
    sweep(pa, pb, fine, goal, 2, wx - 2, 1)
    correct(1, pb)
    for x in range(HX, HX + cells_x):
        v = pb[x, own_y]
        last[x, own_y] = v
        pres_out[x - HX] = v
    l_x[0]()
    s_x[1]()
    l_x[1]()

    mid = slice(HY, HY + cells_y)
    move_x = []
    for x in range(HX - 1, HX + cells_x + 1):
        grad = 0.5 * (last[x + 1, own_y] - last[x - 1, own_y])
        move_x.append(fields[1, x, own_y] - fields[0, x, own_y] * grad)
    for x in range(cells_x):
        w = x + HX
        v = last[w]
        move_y = fields[2, w] - fields[0, w] * (0.5 * (next_y(v) - prev_y(v)))
        own = v[mid]
        dz = jnp.where(lane_o == cells_z - 1, 0.0, next_z(own)) - jnp.where(lane_o == 0, 0.0, prev_z(own))
        move_z = velocity[2, x] - fields[0, w, own_y] * (0.5 * dz)
        vel_out[0, x] = move_x[x + 1]
        vel_out[1, x] = move_y[mid]
        vel_out[2, x] = move_z
        lo_x, hi_x = 0.5 * (move_x[x] + move_x[x + 1]), 0.5 * (move_x[x + 1] + move_x[x + 2])
        lo_y, hi_y = (0.5 * (move_y + prev_y(move_y)))[mid], (0.5 * (move_y + next_y(move_y)))[mid]
        lo_z = 0.5 * (move_z + jnp.where(lane_o == 0, 0.0, prev_z(move_z)))
        hi_z = 0.5 * (move_z + jnp.where(lane_o == cells_z - 1, 0.0, next_z(move_z)))

        def into(flow):
            return time_step * jnp.maximum(flow, 0.0)

        def back(flow):
            return -time_step * jnp.minimum(flow, 0.0)

        keep = 1.0 - (into(hi_x) + into(hi_y) + into(hi_z)) - (back(lo_x) + back(lo_y) + back(lo_z))
        from_xl, from_xu = into(lo_x), back(hi_x)
        from_yl, from_yu = into(lo_y), back(hi_y)
        from_zl = jnp.where(lane_o == 0, 0.0, into(lo_z))
        from_zu = jnp.where(lane_o == cells_z - 1, 0.0, back(hi_z))
        for s in range(species.shape[0]):
            q = species[s, x]
            xl = rim_x[0, s] if x == 0 else species[s, x - 1]
            xu = rim_x[1, s] if x == cells_x - 1 else species[s, x + 1]
            yl = jnp.where(row_o == 0, rim_y[0, s, x, 0:1], prev_y(q))
            yu = jnp.where(row_o == cells_y - 1, rim_y[1, s, x, 0:1], next_y(q))
            total = keep * q + (from_xl * xl + from_xu * xu) + (from_yl * yl + from_yu * yu)
            spec_out[s, x] = total + (from_zl * prev_z(q) + from_zu * next_z(q))

    for x in (f_x, m_x, s_x, r_x[0], p_x, r_x[1], l_x):
        x[2]()


def local(slabs, crosses, velocity, density, source, species):
    cells_x, cells_y, cells_z = density.shape
    assert cells_x == HX and cells_y % HY == 0
    wx, wy = cells_x + 2 * HX, cells_y + 2 * HY
    cw = 5 * cells_x // 2
    kinds = species.shape[0]
    f32 = jnp.float32

    def vmem(*shape):
        return pltpu.VMEM(shape, f32)

    fine, coarse = vmem(wx, wy, cells_z), vmem(cw, wy, cells_z)
    near, wide, side = (pltpu.SemaphoreType.DMA((len(d),)) for d in (NEAR, WIDE, SIDE))
    both = pltpu.SemaphoreType.DMA((CYCLES, len(WIDE)))
    spec = pl.BlockSpec(memory_space=pltpu.VMEM)
    return pl.pallas_call(
        functools.partial(kernel, slabs, crosses),
        out_shape=tuple(jax.ShapeDtypeStruct(a.shape, f32) for a in (velocity, density, species)),
        in_specs=[spec] * 4,
        out_specs=(spec,) * 3,
        scratch_shapes=[
            vmem(4, wx, wy, cells_z), coarse, vmem(CYCLES, cw, wy, cells_z), fine,
            vmem(2, kinds, cells_y, cells_z), vmem(2, kinds, cells_x, 8, cells_z), fine,
            fine, fine, fine, fine, fine, fine, fine, vmem(cells_x, cells_y, cells_z), fine, fine,
            coarse, coarse, coarse, coarse, coarse, coarse, vmem(cells_x // 2, cells_y, cells_z), coarse, coarse,
            near, near, wide, wide, both, both, near, near, side, side, side, side,
        ],
        compiler_params=pltpu.CompilerParams(collective_id=0, has_side_effects=True),
        name="projection",
    )(velocity, density, source, species)


def solution(mesh):
    plane, stack = P("slab", "cross", None), P(None, "slab", "cross", None)
    return jax.shard_map(
        functools.partial(local, mesh.shape["slab"], mesh.shape["cross"]),
        mesh=mesh,
        in_specs=(stack, plane, plane, stack),
        out_specs=(stack, plane, stack),
        check_vma=False,
    )
```

time: 272 us -> 37.1 us (0.14); the launches traced: 267 us -> 36.8 us
  starting transfers between devices: 172 us -> 0 us
  waiting for transfers between devices: 61.6 us -> 0 us
  Pallas kernels: 0 us -> 32.3 us
  other arithmetic: 16 us -> 0 us
  local copies, waits for them, and re-layouts: 15.4 us -> 3.86 us
    ppermute x64 -> x0, starting transfers between devices: 172 us -> none  [the longest x32 131 us: with_halo(): lax.ppermute(lax.slice_in_dim(block, block.shape[dim] - width, None, axis...]
    ppermute x64 -> x0, waiting for transfers between devices: 61.6 us -> none  [the longest x32 51.9 us: with_halo(): lax.ppermute(lax.slice_in_dim(block, 0, width, axis=dim), axis, backward)]
    pallas_call x0 -> x1, Pallas kernels: none -> 32.3 us  [local(): pl.pallas_call(functools.partial(kernel, slabs, crosses), out_shape=tuple...]
    reshape x5 -> x0, local copies, waits for them, and re-layouts: 11.4 us -> none  [the longest x3 7.75 us: restrict(): field.reshape(cells_x // 2, 2, cells_y // 2, 2, cells_z // 2, 2)]
    mul x12 -> x0, other arithmetic: 3.87 us -> none  [the longest x1 1.07 us: local(): (velocity_rim - mobile_rim[None] * gradient(extend(pressure, 2))) * insid...]
    add x16 -> x0, other arithmetic: 3.76 us -> none  [the longest x10 1.74 us: jacobi_step(): return center + damping * (operate(field, weights) - target) / weights[3]]
    div x4 -> x0, other arithmetic: 3.02 us -> none  [the longest x2 2.25 us: jacobi_step(): return center + damping * (operate(field, weights) - target) / weights[3]]
  transfers between devices with their start and end apart: 64 -> 0, of which waited for: 25 -> 0; matrix products, arithmetic and copies ran while one was open for 5% -> 0% of each run, Pallas kernels for 0% -> 0%
where the time goes in v1:
time: 37.1 us; the launch traced here: 36.8 us
  Pallas kernels  32.3 us (87%)
  local copies, waits for them, and re-layouts  3.86 us (10%)
  between operations  0.65 us (2%)
    pallas_call x1, Pallas kernels, local(): pl.pallas_call(functools.partial(kernel, slabs, crosses), out_shape=tuple...  32.3 us
    unnamed x5, local copies, waits for them, and re-layouts  3.86 us

profile of v1, /device:TPU:0, one launch (start us, length us, event | category | flops | bytes accessed | tf_op | source)
XLA Modules:
  0.0 36.8 jit_solution(14870778906772244896)
XLA Ops:
  0.6 32.3 %projection.1 = (f32[3,4,16,128]{3,2,1,0:T(8,128)}, f32[4,16,128]{2,1,0:T(8,128)}, f32[9,4,16,128]{3,2,1,0:T(8,128)}) custom-call(f32[3,4,16,128]{3,2,1,0:T(8,128)} %velocity.1, f32[4,16,128]{2,1,0:T(8,128)} %density.1, f32[4,16,128]{2,1,0:T(8,128)} %source.1, f32[9,4,16,128]{3,2,1,0:T(8,128)} %species.1), custom_call_target="tpu_custom_call" | custom-call | tf_op jit(solution)/shard_map/projection/pallas_call | solution.py:325
  32.9 0.0 copy-start
  32.9 1.5 %copy.10 = f32[3,4,16,128]{3,2,1,0:T(8,128)} copy(f32[3,4,16,128]{3,2,1,0:T(8,128)} %get-tuple-element.6) | data formatting | bytes 196608
  34.5 0.0 copy-done
  34.5 0.6 %copy.11 = f32[4,16,128]{2,1,0:T(8,128)} copy(f32[4,16,128]{2,1,0:T(8,128)S(1)} %copy-done) | data formatting | bytes 65536
  35.1 1.7 %copy.12 = f32[9,4,16,128]{3,2,1,0:T(8,128)} copy(f32[9,4,16,128]{3,2,1,0:T(8,128)} %get-tuple-element.8) | data formatting | bytes 589824
Async XLA Ops:
  32.9 1.6 %copy-start = (f32[4,16,128]{2,1,0:T(8,128)S(1)}, f32[4,16,128]{2,1,0:T(8,128)}, u32[]{:S(2)}) copy-start(f32[4,16,128]{2,1,0:T(8,128)} %get-tuple-element.7) | copy-start | bytes 98308

commit v2 on v1

v2 whole, which is shorter than its diff:
```python
import functools

import jax
import jax.numpy as jnp
from jax import lax
from jax.experimental import pallas as pl
from jax.experimental.pallas import tpu as pltpu
from jax.sharding import PartitionSpec as P

CYCLES = 2
COARSE = 4
damping = 0.8
time_step = 0.25
MESH = pl.DeviceIdType.MESH
RX = 5
RY = 8
CX = 6
CY = 12

NEAR = [(dx, dy) for dx in (-1, 0, 1) for dy in (-1, 0, 1) if (dx, dy) != (0, 0)] + [(-2, 0), (2, 0)]
WIDE = [(dx, dy) for dx in range(-3, 4) for dy in (-1, 0, 1) if (dx, dy) != (0, 0)]
SIDE = [(-1, 0), (1, 0), (0, -1), (0, 1)]
HX, HY = RX, RY


def kernel(
    slabs, crosses, velocity_in, density_in, source_in, species,
    out_x, out_y, out_z, out_p, rim_x, rim_y,
    velocity, density, source, fields, coarse_m, rhs, press,
    xa, xb, ya, yb, za, zb, goal, scale_back, pa, pb,
    cxa, cxb, cya, cyb, cza, czb, cinv, ca, cb, in_sem,
    f_send, f_recv, m_send, m_recv, r_send, r_recv, p_send, p_recv, s_send, s_recv,
):
    cells_x, cells_y, cells_z = density.shape
    wx, wy = cells_x + 2 * HX, cells_y + 2 * HY
    half = cells_x // 2
    cw, cy = half + 2 * CX, cells_y + 2 * CY
    own_y = pl.ds(HY, cells_y)
    own_x = pl.ds(HX, cells_x)
    own_c = pl.ds(CX, half)
    own_cy = pl.ds(CY, cells_y)
    slab, cross = lax.axis_index("slab"), lax.axis_index("cross")
    f32 = jnp.float32

    def there(dx, dy):
        return (slab + dx >= 0) & (slab + dx < slabs) & (cross + dy >= 0) & (cross + dy < crosses)

    def ys(dy, k, rim):
        if dy == 0:
            return pl.ds(rim, cells_y), pl.ds(rim, cells_y)
        if dy > 0:
            return pl.ds(rim + cells_y - k, k), pl.ds(rim - k, k)
        return pl.ds(rim, k), pl.ds(rim + cells_y, k)

    def fine_cut(dx, dy):
        step = max(0, (abs(dx) - 1) * cells_x + 1) if dx != 0 else 0
        k = RX - step
        sy, dyy = ys(dy, k, HY)
        depth = min(cells_x, RX + 1 - step) if dx != 0 else cells_x
        if dx == 0:
            sx, dst_x = own_x, own_x
        elif dx > 0:
            sx, dst_x = pl.ds(HX + cells_x - depth, depth), pl.ds(HX + (1 - dx) * cells_x - depth, depth)
        else:
            sx, dst_x = pl.ds(HX, depth), pl.ds(HX - dx * cells_x, depth)
        return (sx, sy), (dst_x, dyy)

    def coarse_cut(dx, dy):
        step = (abs(dx) - 1) * half + 1 if dx != 0 else 0
        sy, dyy = ys(dy, 2 * (CX - step), CY)
        return (own_c, sy), (pl.ds(CX - dx * half, half), dyy)

    def within(cut, ref, *lead):
        def both(dx, dy):
            src, dst = cut(dx, dy)
            return ref.at[lead + src], ref.at[lead + dst]

        return both

    def exchange(directions, cut, send, recv):
        def copy(index, dx, dy):
            src, dst = cut(dx, dy)
            return pltpu.make_async_remote_copy(
                src_ref=src, dst_ref=dst, send_sem=send.at[index], recv_sem=recv.at[index],
                device_id=(slab + dx, cross + dy), device_id_type=MESH,
            )

        def start():
            for index, (dx, dy) in enumerate(directions):
                @pl.when(there(dx, dy))
                def _():
                    copy(index, dx, dy).start()

        def arrive():
            for index, (dx, dy) in enumerate(directions):
                @pl.when(there(-dx, -dy))
                def _():
                    copy(index, dx, dy).wait_recv()

        def leave():
            for index, (dx, dy) in enumerate(directions):
                @pl.when(there(dx, dy))
                def _():
                    copy(index, dx, dy).wait_send()

        return start, arrive, leave

    f_x = exchange(NEAR, within(fine_cut, fields, slice(None)), f_send, f_recv)
    m_x = exchange(WIDE, within(coarse_cut, coarse_m), m_send, m_recv)
    r_x = [exchange(WIDE, within(coarse_cut, rhs, at), r_send.at[at], r_recv.at[at]) for at in range(CYCLES)]
    p_x = [exchange(NEAR, within(fine_cut, press, at), p_send.at[at], p_recv.at[at]) for at in range(CYCLES)]

    def species_cut(dx, dy):
        if dx != 0:
            return species.at[:, cells_x - 1 if dx > 0 else 0], rim_x.at[0 if dx > 0 else 1]
        return species.at[:, :, cells_y - 1 if dy > 0 else 0], rim_y.at[0 if dy > 0 else 1]

    s_x = exchange(SIDE, species_cut, s_send, s_recv)

    def grids(rows):
        lane = lax.broadcasted_iota(jnp.int32, (rows, cells_z), 1)
        row = lax.broadcasted_iota(jnp.int32, (rows, cells_z), 0)
        return row, lane

    def next_z(v, k=1):
        return pltpu.roll(v, cells_z - k, 1)

    def prev_z(v, k=1):
        return pltpu.roll(v, k, 1)

    def next_y(v, k=1):
        return pltpu.roll(v, v.shape[0] - k, 0)

    def prev_y(v, k=1):
        return pltpu.roll(v, k, 0)

    row_w, lane_w = grids(wy)
    row_c, lane_c = grids(cy)
    row_o, lane_o = grids(cells_y)

    def pair_sum(v, row, lane):
        v = v + jnp.where(row % 2 == 0, next_y(v), prev_y(v))
        return v + jnp.where(lane % 2 == 0, next_z(v), prev_z(v))

    inputs = [
        pltpu.make_async_copy(src, dst, in_sem.at[at])
        for at, (src, dst) in enumerate(((velocity_in, velocity), (density_in, density), (source_in, source)))
    ]
    for copy in inputs:
        copy.start()
    for ref in (fields, coarse_m, rhs, press, rim_x, rim_y):
        ref[...] = jnp.zeros(ref.shape, f32)
    barrier = pltpu.get_barrier_semaphore()
    count = jnp.int32(0)
    for dx, dy in WIDE:
        here = there(dx, dy)
        count = count + here.astype(jnp.int32)

        @pl.when(here)
        def _():
            pl.semaphore_signal(barrier, inc=1, device_id=(slab + dx, cross + dy), device_id_type=MESH)

    for copy in inputs:
        copy.wait()
    for x in range(cells_x):
        v2 = velocity[2, x]
        dz = jnp.where(lane_o == cells_z - 1, 0.0, next_z(v2)) - jnp.where(lane_o == 0, 0.0, prev_z(v2))
        fields[0, HX + x, own_y] = 1.0 / density[x]
        fields[1, HX + x, own_y] = velocity[0, x]
        fields[2, HX + x, own_y] = velocity[1, x]
        fields[3, HX + x, own_y] = 0.5 * dz - source[x]
    for c in range(half):
        m = 1.0 / density[2 * c] + 1.0 / density[2 * c + 1]
        coarse_m[CX + c, own_cy] = 0.125 * pair_sum(m, row_o, lane_o)
    pl.semaphore_wait(barrier, count)
    f_x[0]()
    m_x[0]()
    s_x[0]()
    f_x[1]()

    for x in range(1, wx - 1):
        m = fields[0, x]
        lo_x, hi_x = 0.5 * (m + fields[0, x - 1]), 0.5 * (m + fields[0, x + 1])
        lo_y, hi_y = 0.5 * (m + prev_y(m)), 0.5 * (m + next_y(m))
        lo_z = 0.5 * (m + jnp.where(lane_w == 0, 0.0, prev_z(m)))
        hi_z = 0.5 * (m + jnp.where(lane_w == cells_z - 1, 0.0, next_z(m)))
        diag = lo_x + hi_x + lo_y + hi_y + lo_z + hi_z
        inside = m > 0.0
        inv = jnp.where(inside, damping / jnp.where(inside, diag, 1.0), 0.0)
        xa[x], xb[x] = lo_x * inv, hi_x * inv
        ya[x], yb[x] = lo_y * inv, hi_y * inv
        za[x] = jnp.where(lane_w == 0, 0.0, lo_z * inv)
        zb[x] = jnp.where(lane_w == cells_z - 1, 0.0, hi_z * inv)
        if HX <= x < HX + cells_x:
            scale_back[x - HX] = (diag * (1.0 / damping))[HY : HY + cells_y]
        v1 = fields[2, x]
        t = 0.5 * ((fields[1, x + 1] - fields[1, x - 1]) + (next_y(v1) - prev_y(v1))) + fields[3, x]
        b = t * inv
        goal[x] = b
        pa[x] = -b

    def sweep(src, dst, coefs, right, low, high, k):
        xl, xu, yl, yu, zl, zu = coefs
        for x in range(low, high):
            v = src[x]
            t = xl[x] * src[x - 1] + xu[x] * src[x + 1]
            t = t + (yl[x] * prev_y(v, k) + yu[x] * next_y(v, k))
            t = t + (zl[x] * prev_z(v, k) + zu[x] * next_z(v, k))
            dst[x] = (1.0 - damping) * v + (t - right[x])

    fine = (xa, xb, ya, yb, za, zb)
    coarse = (cxa, cxb, cya, cyb, cza, czb)

    def coarse_setup():
        for x in range(1, cw - 1):
            m = coarse_m[x]
            lo_x, hi_x = 0.5 * (m + coarse_m[x - 1]), 0.5 * (m + coarse_m[x + 1])
            lo_y, hi_y = 0.5 * (m + prev_y(m, 2)), 0.5 * (m + next_y(m, 2))
            lo_z = 0.5 * (m + jnp.where(lane_c < 2, 0.0, prev_z(m, 2)))
            hi_z = 0.5 * (m + jnp.where(lane_c >= cells_z - 2, 0.0, next_z(m, 2)))
            diag = lo_x + hi_x + lo_y + hi_y + lo_z + hi_z
            inside = m > 0.0
            inv = jnp.where(inside, damping / jnp.where(inside, diag, 1.0), 0.0)
            cxa[x], cxb[x] = lo_x * inv, hi_x * inv
            cya[x], cyb[x] = lo_y * inv, hi_y * inv
            cza[x] = jnp.where(lane_c < 2, 0.0, lo_z * inv)
            czb[x] = jnp.where(lane_c >= cells_z - 2, 0.0, hi_z * inv)
            if CX <= x < CX + half:
                cinv[x - CX] = inv[CY : CY + cells_y]

    def correct(at, pre, free, reach):
        for x in range(HX, HX + cells_x):
            press[at, x, own_y] = pre[x, own_y]
        p_x[at][0]()
        if at == 0:
            m_x[1]()
            coarse_setup()
        for c in range(half):
            r = None
            for x in (HX + 2 * c, HX + 2 * c + 1):
                v = pre[x]
                t = xa[x] * pre[x - 1] + xb[x] * pre[x + 1]
                t = t + (ya[x] * prev_y(v) + yb[x] * next_y(v))
                t = t + (za[x] * prev_z(v) + zb[x] * next_z(v))
                d = (damping * v - (t - goal[x]))[HY : HY + cells_y] * scale_back[x - HX]
                r = d if r is None else r + d
            rhs[at, CX + c, own_cy] = 0.5 * pair_sum(r, row_o, lane_o) * cinv[c]
        r_x[at][0]()
        r_x[at][1]()
        right = rhs.at[at]
        for x in range(cw):
            ca[x] = -right[x]
        src, dst = ca, cb
        for step in range(1, COARSE):
            sweep(src, dst, coarse, right, step, cw - step, 2)
            src, dst = dst, src
        p_x[at][1]()
        low, high = HX - reach - 2, HX + cells_x + reach + 2
        for x in range(low, high):
            pre[x] = press[at, x] + src[CX + (x - HX) // 2, pl.ds(CY - HY, wy)]
        sweep(pre, free, fine, goal, low + 1, high - 1, 1)
        sweep(free, pre, fine, goal, low + 2, high - 2, 1)

    sweep(pa, pb, fine, goal, HX - 1, HX + cells_x + 1, 1)
    correct(0, pb, pa, 3)
    sweep(pb, pa, fine, goal, HX - 2, HX + cells_x + 2, 1)
    sweep(pa, pb, fine, goal, HX - 1, HX + cells_x + 1, 1)
    correct(1, pb, pa, 2)
    last = pb

    for x in range(HX - 1, HX + cells_x + 1):
        grad = 0.5 * (last[x + 1, own_y] - last[x - 1, own_y])
        out_x[x - HX + 1] = fields[1, x, own_y] - fields[0, x, own_y] * grad
    for x in range(cells_x):
        w = x + HX
        v = last[w]
        out_y[x] = fields[2, w] - fields[0, w] * (0.5 * (next_y(v) - prev_y(v)))
        own = v[HY : HY + cells_y]
        dz = jnp.where(lane_o == cells_z - 1, 0.0, next_z(own)) - jnp.where(lane_o == 0, 0.0, prev_z(own))
        out_z[x] = velocity[2, x] - fields[0, w, own_y] * (0.5 * dz)
        out_p[x] = own
    s_x[1]()
    for x in (f_x, m_x, s_x, *r_x, *p_x):
        x[2]()


def transport(in_x, in_y, in_z, in_p, rim_x, rim_y, species, vel_out, pres_out, spec_out):
    cells_x, cells_y, cells_z = in_p.shape
    lane_o = lax.broadcasted_iota(jnp.int32, (cells_y, cells_z), 1)
    row_o = lax.broadcasted_iota(jnp.int32, (cells_y, cells_z), 0)

    def next_z(v):
        return pltpu.roll(v, cells_z - 1, 1)

    def prev_z(v):
        return pltpu.roll(v, 1, 1)

    def next_y(v):
        return pltpu.roll(v, v.shape[0] - 1, 0)

    def prev_y(v):
        return pltpu.roll(v, 1, 0)

    mid = slice(HY, HY + cells_y)
    pres_out[...] = in_p[...]
    move_x = [in_x[x] for x in range(cells_x + 2)]
    for x in range(cells_x):
        move_y, move_z = in_y[x], in_z[x]
        vel_out[0, x] = move_x[x + 1]
        vel_out[1, x] = move_y[mid]
        vel_out[2, x] = move_z
        lo_x, hi_x = 0.5 * (move_x[x] + move_x[x + 1]), 0.5 * (move_x[x + 1] + move_x[x + 2])
        lo_y, hi_y = (0.5 * (move_y + prev_y(move_y)))[mid], (0.5 * (move_y + next_y(move_y)))[mid]
        lo_z = 0.5 * (move_z + jnp.where(lane_o == 0, 0.0, prev_z(move_z)))
        hi_z = 0.5 * (move_z + jnp.where(lane_o == cells_z - 1, 0.0, next_z(move_z)))

        def into(flow):
            return time_step * jnp.maximum(flow, 0.0)

        def back(flow):
            return -time_step * jnp.minimum(flow, 0.0)

        keep = 1.0 - (into(hi_x) + into(hi_y) + into(hi_z)) - (back(lo_x) + back(lo_y) + back(lo_z))
        from_xl, from_xu = into(lo_x), back(hi_x)
        from_yl, from_yu = into(lo_y), back(hi_y)
        from_zl = jnp.where(lane_o == 0, 0.0, into(lo_z))
        from_zu = jnp.where(lane_o == cells_z - 1, 0.0, back(hi_z))
        for s in range(species.shape[0]):
            q = species[s, x]
            xl = rim_x[0, s] if x == 0 else species[s, x - 1]
            xu = rim_x[1, s] if x == cells_x - 1 else species[s, x + 1]
            yl = jnp.where(row_o == 0, rim_y[0, s, pl.ds(x, 1)], prev_y(q))
            yu = jnp.where(row_o == cells_y - 1, rim_y[1, s, pl.ds(x, 1)], next_y(q))
            total = keep * q + (from_xl * xl + from_xu * xu) + (from_yl * yl + from_yu * yu)
            spec_out[s, x] = total + (from_zl * prev_z(q) + from_zu * next_z(q))


def local(slabs, crosses, velocity, density, source, species):
    cells_x, cells_y, cells_z = density.shape
    assert cells_x == 4 and cells_y % 8 == 0 and cells_y >= CY
    wx, wy = cells_x + 2 * HX, cells_y + 2 * HY
    half = cells_x // 2
    kinds = species.shape[0]
    f32 = jnp.float32

    def vmem(*shape):
        return pltpu.VMEM(shape, f32)

    fine, coarse = (wx, wy, cells_z), (half + 2 * CX, cells_y + 2 * CY, cells_z)
    near, wide, side = len(NEAR), len(WIDE), len(SIDE)
    dma = pltpu.SemaphoreType.DMA
    spec = pl.BlockSpec(memory_space=pltpu.VMEM)
    anywhere = pl.BlockSpec(memory_space=pl.ANY)
    moved = [
        (cells_x + 2, cells_y, cells_z), (cells_x, wy, cells_z), density.shape, density.shape,
        (2, kinds, cells_y, cells_z), (2, kinds, cells_x, cells_z),
    ]
    between = pl.pallas_call(
        functools.partial(kernel, slabs, crosses),
        out_shape=tuple(jax.ShapeDtypeStruct(shape, f32) for shape in moved),
        in_specs=[anywhere] * 4,
        out_specs=(spec,) * 6,
        scratch_shapes=[vmem(*velocity.shape), vmem(*density.shape), vmem(*density.shape)]
        + [vmem(4, *fine), vmem(*coarse), vmem(CYCLES, *coarse), vmem(CYCLES, *fine)]
        + [vmem(*fine)] * 7 + [vmem(*density.shape)] + [vmem(*fine)] * 2
        + [vmem(*coarse)] * 6 + [vmem(half, cells_y, cells_z)] + [vmem(*coarse)] * 2
        + [dma((3,))] + [dma((near,))] * 2 + [dma((wide,))] * 2
        + [dma((CYCLES, wide))] * 2 + [dma((CYCLES, near))] * 2 + [dma((side,))] * 2,
        compiler_params=pltpu.CompilerParams(collective_id=0, has_side_effects=True),
        name="projection",
    )(velocity, density, source, species)
    return pl.pallas_call(
        transport,
        out_shape=tuple(jax.ShapeDtypeStruct(a.shape, f32) for a in (velocity, density, species)),
        in_specs=[spec] * 7,
        out_specs=(spec,) * 3,
        name="transport",
    )(*between, species)


def solution(mesh):
    plane, stack = P("slab", "cross", None), P(None, "slab", "cross", None)
    return jax.shard_map(
        functools.partial(local, mesh.shape["slab"], mesh.shape["cross"]),
        mesh=mesh,
        in_specs=(stack, plane, plane, stack),
        out_specs=(stack, plane, stack),
        check_vma=False,
    )
```

time: 37.1 us -> 31.8 us (0.86)
  local copies, waits for them, and re-layouts: 3.86 us -> 0 us
  Pallas kernels: 32.3 us -> 31 us
    unnamed x5 -> x0, local copies, waits for them, and re-layouts: 3.86 us -> none
    pallas_call x1, Pallas kernels: 32.3 us -> 28.8 us  [local(): pl.pallas_call(functools.partial(kernel, slabs, crosses), out_shape=tuple...]
    pallas_call x0 -> x1, Pallas kernels: none -> 2.17 us  [local(): pl.pallas_call(transport, out_shape=tuple((jax.ShapeDtypeStruct(a.shape,...]
where the time goes in v2:
time: 31.8 us; the launch traced here: 31.6 us
  Pallas kernels  31 us (97%)
  between operations  0.64 us (2%)
    pallas_call x1, Pallas kernels, local(): pl.pallas_call(functools.partial(kernel, slabs, crosses), out_shape=tuple...  28.8 us
    pallas_call x1, Pallas kernels, local(): pl.pallas_call(transport, out_shape=tuple((jax.ShapeDtypeStruct(a.shape,...  2.17 us

profile of v2, /device:TPU:0, one launch (start us, length us, event | category | flops | bytes accessed | tf_op | source)
XLA Modules:
  0.0 31.6 jit_solution(7347116980716589278)
XLA Ops:
  0.6 28.8 %projection.1 = (f32[6,16,128]{2,1,0:T(8,128)}, f32[4,32,128]{2,1,0:T(8,128)}, f32[4,16,128]{2,1,0:T(8,128)}, f32[4,16,128]{2,1,0:T(8,128)}, f32[2,9,16,128]{3,2,1,0:T(8,128)}, /*index=5*/f32[2,9,4,128]{3,2,1,0:T(4,128)}) custom-call(f32[3,4,16,128]{3,2,1,0:T(8,128)} %velocity_in.1, f32[4,16,128]{2,1,0:T(8,128)} %density_in.1, f32[4,16,128]{2,1,0:T(8,128)} %source_in.1, ...), custom_call_target="tpu_custom_call" | custom-call | tf_op jit(solution)/shard_map/projection/pallas_call | solution.py:358
  29.5 2.2 %transport.1 = (f32[3,4,16,128]{3,2,1,0:T(8,128)}, f32[4,16,128]{2,1,0:T(8,128)}, f32[9,4,16,128]{3,2,1,0:T(8,128)}) custom-call(f32[6,16,128]{2,1,0:T(8,128)} %get-tuple-element.9.in_x, f32[4,32,128]{2,1,0:T(8,128)} %get-tuple-element.10.in_y, f32[4,16,128]{2,1,0:T(8,128)} %get-tuple-element.11.in_z, f32[4,16,128]{2,1,0:T(8,128)} %get-tuple-element.12.in_p, ...), custom_call_target="tpu_custom_call" | custom-call | tf_op jit(solution)/shard_map/transport/pallas_call | solution.py:372

commit v3 on v2

--- a/solution.py
+++ b/solution.py
@@ -26,7 +26,7 @@
 def kernel(
     slabs, crosses, velocity_in, density_in, source_in, species,
     out_x, out_y, out_z, out_p, rim_x, rim_y,
-    velocity, density, source, fields, coarse_m, rhs, press,
+    velocity, density, source, fields, packed_m, packed_r, press, coarse_m, right,
     xa, xb, ya, yb, za, zb, goal, scale_back, pa, pb,
     cxa, cxb, cya, cyb, cza, czb, cinv, ca, cb, in_sem,
     f_send, f_recv, m_send, m_recv, r_send, r_recv, p_send, p_recv, s_send, s_recv,
@@ -37,7 +37,6 @@
     cw, cy = half + 2 * CX, cells_y + 2 * CY
     own_y = pl.ds(HY, cells_y)
     own_x = pl.ds(HX, cells_x)
-    own_c = pl.ds(CX, half)
     own_cy = pl.ds(CY, cells_y)
     slab, cross = lax.axis_index("slab"), lax.axis_index("cross")
     f32 = jnp.float32
@@ -68,7 +67,7 @@
     def coarse_cut(dx, dy):
         step = (abs(dx) - 1) * half + 1 if dx != 0 else 0
         sy, dyy = ys(dy, 2 * (CX - step), CY)
-        return (own_c, sy), (pl.ds(CX - dx * half, half), dyy)
+        return (CX // half, sy), (CX // half - dx, dyy)
 
     def within(cut, ref, *lead):
         def both(dx, dy):
@@ -105,9 +104,12 @@
 
         return start, arrive, leave
 
-    f_x = exchange(NEAR, within(fine_cut, fields, slice(None)), f_send, f_recv)
-    m_x = exchange(WIDE, within(coarse_cut, coarse_m), m_send, m_recv)
-    r_x = [exchange(WIDE, within(coarse_cut, rhs, at), r_send.at[at], r_recv.at[at]) for at in range(CYCLES)]
+    def fields_cut(dx, dy):
+        return within(fine_cut, fields, slice(0, 2) if abs(dx) > 1 else slice(None))(dx, dy)
+
+    f_x = exchange(NEAR, fields_cut, f_send, f_recv)
+    m_x = exchange(WIDE, within(coarse_cut, packed_m), m_send, m_recv)
+    r_x = [exchange(WIDE, within(coarse_cut, packed_r, at), r_send.at[at], r_recv.at[at]) for at in range(CYCLES)]
     p_x = [exchange(NEAR, within(fine_cut, press, at), p_send.at[at], p_recv.at[at]) for at in range(CYCLES)]
 
     def species_cut(dx, dy):
@@ -141,6 +143,15 @@
     def pair_sum(v, row, lane):
         v = v + jnp.where(row % 2 == 0, next_y(v), prev_y(v))
         return v + jnp.where(lane % 2 == 0, next_z(v), prev_z(v))
+
+    def pack(two):
+        return jnp.where(lane_o % 2 == 0, two[0], two[1])
+
+    def unpack(ref, dst):
+        for block in range(2 * CX // half + 1):
+            e = ref[block]
+            dst[2 * block] = jnp.where(lane_c % 2 == 0, e, prev_z(e))
+            dst[2 * block + 1] = jnp.where(lane_c % 2 == 0, next_z(e), e)
 
     inputs = [
         pltpu.make_async_copy(src, dst, in_sem.at[at])
@@ -148,7 +159,7 @@
     ]
     for copy in inputs:
         copy.start()
-    for ref in (fields, coarse_m, rhs, press, rim_x, rim_y):
+    for ref in (fields, packed_m, packed_r, press, rim_x, rim_y):
         ref[...] = jnp.zeros(ref.shape, f32)
     barrier = pltpu.get_barrier_semaphore()
     count = jnp.int32(0)
@@ -169,35 +180,41 @@
         fields[1, HX + x, own_y] = velocity[0, x]
         fields[2, HX + x, own_y] = velocity[1, x]
         fields[3, HX + x, own_y] = 0.5 * dz - source[x]
+    means = []
     for c in range(half):
         m = 1.0 / density[2 * c] + 1.0 / density[2 * c + 1]
-        coarse_m[CX + c, own_cy] = 0.125 * pair_sum(m, row_o, lane_o)
+        means.append(0.125 * pair_sum(m, row_o, lane_o))
+    packed_m[CX // half, own_cy] = pack(means)
     pl.semaphore_wait(barrier, count)
     f_x[0]()
     m_x[0]()
     s_x[0]()
     f_x[1]()
 
-    for x in range(1, wx - 1):
-        m = fields[0, x]
-        lo_x, hi_x = 0.5 * (m + fields[0, x - 1]), 0.5 * (m + fields[0, x + 1])
-        lo_y, hi_y = 0.5 * (m + prev_y(m)), 0.5 * (m + next_y(m))
-        lo_z = 0.5 * (m + jnp.where(lane_w == 0, 0.0, prev_z(m)))
-        hi_z = 0.5 * (m + jnp.where(lane_w == cells_z - 1, 0.0, next_z(m)))
-        diag = lo_x + hi_x + lo_y + hi_y + lo_z + hi_z
-        inside = m > 0.0
-        inv = jnp.where(inside, damping / jnp.where(inside, diag, 1.0), 0.0)
-        xa[x], xb[x] = lo_x * inv, hi_x * inv
-        ya[x], yb[x] = lo_y * inv, hi_y * inv
-        za[x] = jnp.where(lane_w == 0, 0.0, lo_z * inv)
-        zb[x] = jnp.where(lane_w == cells_z - 1, 0.0, hi_z * inv)
-        if HX <= x < HX + cells_x:
-            scale_back[x - HX] = (diag * (1.0 / damping))[HY : HY + cells_y]
-        v1 = fields[2, x]
-        t = 0.5 * ((fields[1, x + 1] - fields[1, x - 1]) + (next_y(v1) - prev_y(v1))) + fields[3, x]
-        b = t * inv
-        goal[x] = b
-        pa[x] = -b
+    def fine_setup(rows):
+        for x in rows:
+            m = fields[0, x]
+            lo_x, hi_x = 0.5 * (m + fields[0, x - 1]), 0.5 * (m + fields[0, x + 1])
+            lo_y, hi_y = 0.5 * (m + prev_y(m)), 0.5 * (m + next_y(m))
+            lo_z = 0.5 * (m + jnp.where(lane_w == 0, 0.0, prev_z(m)))
+            hi_z = 0.5 * (m + jnp.where(lane_w == cells_z - 1, 0.0, next_z(m)))
+            diag = lo_x + hi_x + lo_y + hi_y + lo_z + hi_z
+            inside = m > 0.0
+            inv = jnp.where(inside, damping / jnp.where(inside, diag, 1.0), 0.0)
+            xa[x], xb[x] = lo_x * inv, hi_x * inv
+            ya[x], yb[x] = lo_y * inv, hi_y * inv
+            za[x] = jnp.where(lane_w == 0, 0.0, lo_z * inv)
+            zb[x] = jnp.where(lane_w == cells_z - 1, 0.0, hi_z * inv)
+            if HX <= x < HX + cells_x:
+                scale_back[x - HX] = (diag * (1.0 / damping))[HY : HY + cells_y]
+            v1 = fields[2, x]
+            t = 0.5 * ((fields[1, x + 1] - fields[1, x - 1]) + (next_y(v1) - prev_y(v1))) + fields[3, x]
+            b = t * inv
+            goal[x] = b
+            pa[x] = -b
+
+    early = range(HX - 2, HX + cells_x + 2)
+    fine_setup(early)
 
     def sweep(src, dst, coefs, right, low, high, k):
         xl, xu, yl, yu, zl, zu = coefs
@@ -211,8 +228,8 @@
     fine = (xa, xb, ya, yb, za, zb)
     coarse = (cxa, cxb, cya, cyb, cza, czb)
 
-    def coarse_setup():
-        for x in range(1, cw - 1):
+    def coarse_setup(rows):
+        for x in rows:
             m = coarse_m[x]
             lo_x, hi_x = 0.5 * (m + coarse_m[x - 1]), 0.5 * (m + coarse_m[x + 1])
             lo_y, hi_y = 0.5 * (m + prev_y(m, 2)), 0.5 * (m + next_y(m, 2))
@@ -231,10 +248,12 @@
     def correct(at, pre, free, reach):
         for x in range(HX, HX + cells_x):
             press[at, x, own_y] = pre[x, own_y]
-        p_x[at][0]()
+        own_rows = range(CX, CX + half)
         if at == 0:
             m_x[1]()
-            coarse_setup()
+            unpack(packed_m, coarse_m)
+            coarse_setup(own_rows)
+        sums = []
         for c in range(half):
             r = None
             for x in (HX + 2 * c, HX + 2 * c + 1):
@@ -244,10 +263,15 @@
                 t = t + (za[x] * prev_z(v) + zb[x] * next_z(v))
                 d = (damping * v - (t - goal[x]))[HY : HY + cells_y] * scale_back[x - HX]
                 r = d if r is None else r + d
-            rhs[at, CX + c, own_cy] = 0.5 * pair_sum(r, row_o, lane_o) * cinv[c]
+            sums.append(0.5 * pair_sum(r, row_o, lane_o) * cinv[c])
+        packed_r[at, CX // half, own_cy] = pack(sums)
         r_x[at][0]()
+        p_x[at][0]()
+        if at == 0:
+            coarse_setup([x for x in range(1, cw - 1) if x not in own_rows])
+            fine_setup([x for x in range(1, wx - 1) if x not in early])
         r_x[at][1]()
-        right = rhs.at[at]
+        unpack(packed_r.at[at], right)
         for x in range(cw):
             ca[x] = -right[x]
         src, dst = ca, cb
@@ -337,7 +361,7 @@
 
 def local(slabs, crosses, velocity, density, source, species):
     cells_x, cells_y, cells_z = density.shape
-    assert cells_x == 4 and cells_y % 8 == 0 and cells_y >= CY
+    assert cells_x == 4 and CX % (cells_x // 2) == 0 and cells_y % 8 == 0 and cells_y >= CY
     wx, wy = cells_x + 2 * HX, cells_y + 2 * HY
     half = cells_x // 2
     kinds = species.shape[0]
@@ -347,6 +371,7 @@
         return pltpu.VMEM(shape, f32)
 
     fine, coarse = (wx, wy, cells_z), (half + 2 * CX, cells_y + 2 * CY, cells_z)
+    packed = (2 * CX // half + 1,) + coarse[1:]
     near, wide, side = len(NEAR), len(WIDE), len(SIDE)
     dma = pltpu.SemaphoreType.DMA
     spec = pl.BlockSpec(memory_space=pltpu.VMEM)
@@ -361,7 +386,8 @@
         in_specs=[anywhere] * 4,
         out_specs=(spec,) * 6,
         scratch_shapes=[vmem(*velocity.shape), vmem(*density.shape), vmem(*density.shape)]
-        + [vmem(4, *fine), vmem(*coarse), vmem(CYCLES, *coarse), vmem(CYCLES, *fine)]
+        + [vmem(4, *fine), vmem(*packed), vmem(CYCLES, *packed), vmem(CYCLES, *fine)]
+        + [vmem(*coarse)] * 2
         + [vmem(*fine)] * 7 + [vmem(*density.shape)] + [vmem(*fine)] * 2
         + [vmem(*coarse)] * 6 + [vmem(half, cells_y, cells_z)] + [vmem(*coarse)] * 2
         + [dma((3,))] + [dma((near,))] * 2 + [dma((wide,))] * 2

time: 31.8 us -> 28.9 us (0.909)
  Pallas kernels: 31 us -> 28.1 us
    pallas_call x1, Pallas kernels: 28.8 us -> 25.9 us  [local(): pl.pallas_call(functools.partial(kernel, slabs, crosses), out_shape=tuple...]
where the time goes in v3:
time: 28.9 us; the launch traced here: 28.8 us
  Pallas kernels  28.1 us (97%)
  between operations  0.64 us (2%)
    pallas_call x1, Pallas kernels, local(): pl.pallas_call(functools.partial(kernel, slabs, crosses), out_shape=tuple...  25.9 us
    pallas_call x1, Pallas kernels, local(): pl.pallas_call(transport, out_shape=tuple((jax.ShapeDtypeStruct(a.shape,...  2.17 us

profile of v3, /device:TPU:0, one launch (start us, length us, event | category | flops | bytes accessed | tf_op | source)
XLA Modules:
  0.0 28.8 jit_solution(10334221446103131715)
XLA Ops:
  0.6 25.9 %projection.1 = (f32[6,16,128]{2,1,0:T(8,128)}, f32[4,32,128]{2,1,0:T(8,128)}, f32[4,16,128]{2,1,0:T(8,128)}, f32[4,16,128]{2,1,0:T(8,128)}, f32[2,9,16,128]{3,2,1,0:T(8,128)}, /*index=5*/f32[2,9,4,128]{3,2,1,0:T(4,128)}) custom-call(f32[3,4,16,128]{3,2,1,0:T(8,128)} %velocity_in.1, f32[4,16,128]{2,1,0:T(8,128)} %density_in.1, f32[4,16,128]{2,1,0:T(8,128)} %source_in.1, ...), custom_call_target="tpu_custom_call" | custom-call | tf_op jit(solution)/shard_map/projection/pallas_call | solution.py:383
  26.6 2.2 %transport.1 = (f32[3,4,16,128]{3,2,1,0:T(8,128)}, f32[4,16,128]{2,1,0:T(8,128)}, f32[9,4,16,128]{3,2,1,0:T(8,128)}) custom-call(f32[6,16,128]{2,1,0:T(8,128)} %get-tuple-element.9.in_x, f32[4,32,128]{2,1,0:T(8,128)} %get-tuple-element.10.in_y, f32[4,16,128]{2,1,0:T(8,128)} %get-tuple-element.11.in_z, f32[4,16,128]{2,1,0:T(8,128)} %get-tuple-element.12.in_p, ...), custom_call_target="tpu_custom_call" | custom-call | tf_op jit(solution)/shard_map/transport/pallas_call | solution.py:398

commit v4 on v3

--- a/solution.py
+++ b/solution.py
@@ -188,7 +188,6 @@
     pl.semaphore_wait(barrier, count)
     f_x[0]()
     m_x[0]()
-    s_x[0]()
     f_x[1]()
 
     def fine_setup(rows):
@@ -268,6 +267,7 @@
         r_x[at][0]()
         p_x[at][0]()
         if at == 0:
+            s_x[0]()
             coarse_setup([x for x in range(1, cw - 1) if x not in own_rows])
             fine_setup([x for x in range(1, wx - 1) if x not in early])
         r_x[at][1]()

time: 28.9 us -> 29 us (level)
  no operation moved by 1% of the time
where the time goes in v4:
time: 29 us; the launch traced here: 28.8 us
  Pallas kernels  28.2 us (97%)
  between operations  0.64 us (2%)
    pallas_call x1, Pallas kernels, local(): pl.pallas_call(functools.partial(kernel, slabs, crosses), out_shape=tuple...  26 us
    pallas_call x1, Pallas kernels, local(): pl.pallas_call(transport, out_shape=tuple((jax.ShapeDtypeStruct(a.shape,...  2.17 us

profile of v4, /device:TPU:0, one launch (start us, length us, event | category | flops | bytes accessed | tf_op | source)
XLA Modules:
  0.0 28.8 jit_solution(5123064557279708464)
XLA Ops:
  0.6 26.0 %projection.1 = (f32[6,16,128]{2,1,0:T(8,128)}, f32[4,32,128]{2,1,0:T(8,128)}, f32[4,16,128]{2,1,0:T(8,128)}, f32[4,16,128]{2,1,0:T(8,128)}, f32[2,9,16,128]{3,2,1,0:T(8,128)}, /*index=5*/f32[2,9,4,128]{3,2,1,0:T(4,128)}) custom-call(f32[3,4,16,128]{3,2,1,0:T(8,128)} %velocity_in.1, f32[4,16,128]{2,1,0:T(8,128)} %density_in.1, f32[4,16,128]{2,1,0:T(8,128)} %source_in.1, ...), custom_call_target="tpu_custom_call" | custom-call | tf_op jit(solution)/shard_map/projection/pallas_call | solution.py:383
  26.6 2.2 %transport.1 = (f32[3,4,16,128]{3,2,1,0:T(8,128)}, f32[4,16,128]{2,1,0:T(8,128)}, f32[9,4,16,128]{3,2,1,0:T(8,128)}) custom-call(f32[6,16,128]{2,1,0:T(8,128)} %get-tuple-element.9.in_x, f32[4,32,128]{2,1,0:T(8,128)} %get-tuple-element.10.in_y, f32[4,16,128]{2,1,0:T(8,128)} %get-tuple-element.11.in_z, f32[4,16,128]{2,1,0:T(8,128)} %get-tuple-element.12.in_p, ...), custom_call_target="tpu_custom_call" | custom-call | tf_op jit(solution)/shard_map/transport/pallas_call | solution.py:398
